TPU v7x, 256 devices: a whole 4x4x8 slice. The times are simulated.
256 devices in a mesh: dp: 16 (over x_lo, y, core), tp: 16 (over z, x_hi).
Axes of the slice: x: 4 (x_hi: 2, x_lo: 2; x = x_hi * 2 + x_lo), y: 4, z: 8, core: 2. Of those that a mesh axis runs over, the one named last changes fastest.
Arguments:
- inputs: bfloat16 [16, 3072, 1280], P('dp', 'tp'), may hold values from -6 to 6
- saved_hidden: bfloat16 [16, 3072, 5120], P('dp', None, 'tp'), may hold values from -8 to 8
- upstream: bfloat16 [16, 3072, 1280], P('dp', 'tp'), may hold values from -6 to 6
- w_in: bfloat16 [1280, 5120], P(None, 'tp'), may hold values from -0.15625 to 0.15625
- w_out: bfloat16 [5120, 1280], P('tp'), may hold values from -0.078125 to 0.078125
- kernel: float32 [7, 1280], replicated, may hold values from -2 to 2
Outputs:
- grad_inputs: bfloat16 [16, 3072, 1280], P('dp', 'tp')
- grad_w_in: float32 [1280, 5120], P(None, 'tp')
- grad_w_out: float32 [5120, 1280], P('tp')
- grad_bias: float32 [5120], P('tp')
- grad_kernel: float32 [7, 1280], replicated
All inputs are finite; a program needn't handle non-finite values.
Results may differ from a plain program's by a relative error of at most 0.02.
Values may be sent and summed in bfloat16 or wider, within the bound.
A program may use at most 128 MiB of HBM per device.

v0:
```python
import jax
import jax.numpy as jnp
from jax import lax
from jax.sharding import Mesh
from jax.sharding import PartitionSpec as P

KW = 7
TP = ("tp_0", "tp_1")


def own_rows(terms, axes):
    running = terms.astype(jnp.bfloat16)
    for axis in axes:
        running = lax.psum_scatter(running, axis, scatter_dimension=0, tiled=True)
    return running.astype(jnp.float32)


def with_halo(cells, sides, width):
    for axis, dim in sides:
        count = lax.axis_size(axis)
        ends = count - 1
        head = lax.slice_in_dim(cells, 0, width, axis=dim)
        tail = lax.slice_in_dim(cells, cells.shape[dim] - width, cells.shape[dim], axis=dim)
        cells = jnp.concatenate(
            [
                lax.ppermute(tail, axis, [(i, (i + 1) % count) for i in range(ends)]),
                cells,
                lax.ppermute(head, axis, [((i + 1) % count, i) for i in range(ends)]),
            ],
            axis=dim,
        )
    return cells


def sent_to_all(array, axis):
    copies = jnp.broadcast_to(array, (lax.axis_size(axis), *array.shape))
    return lax.all_to_all(copies, axis, split_axis=0, concat_axis=0, tiled=True)


def over_copies(array, axis):
    return sent_to_all(array, axis).astype(jnp.float32).sum(axis=0)


def gelu_exact(value):
    return jax.nn.gelu(value, approximate=False)


def convolve(padded, kernel, length):
    mixed = padded[3 : 3 + length].astype(jnp.float32)
    for tap in range(KW):
        mixed = mixed + kernel[tap] * padded[tap : tap + length].astype(jnp.float32)
    return mixed.astype(jnp.bfloat16)


def shards(inputs, saved_hidden, upstream, w_in, w_out, kernel):
    tokens = inputs[0]
    hidden = saved_hidden[0]
    grad_out = upstream[0]
    length = tokens.shape[0]
    seq_len = hidden.shape[0]
    piece = lax.all_gather(grad_out, TP, axis=0, tiled=True)
    hidden_rows = hidden.astype(jnp.float32)
    back_rows = lax.dot_general(
        piece, w_out, (((1,), (1,)), ((), ())), preferred_element_type=jnp.float32
    )
    grad_rows = jax.vjp(gelu_exact, hidden_rows)[1](back_rows)[0].astype(jnp.bfloat16)
    activated = gelu_exact(hidden_rows).astype(jnp.bfloat16)
    total = lax.dot_general(
        activated, piece, (((0,), (0,)), ((), ())), preferred_element_type=jnp.float32
    )
    grad_w_out = total
    grad_bias = jnp.sum(grad_rows.astype(jnp.float32), axis=0)
    summed = own_rows(
        lax.dot_general(
            grad_rows, w_in, (((1,), (1,)), ((), ())), preferred_element_type=jnp.float32
        ),
        TP,
    )
    grad_mixed = (grad_out.astype(jnp.float32) + summed).astype(jnp.bfloat16)
    gathered = lax.all_gather(tokens, TP, axis=0, tiled=True)
    whole_pad = jnp.pad(gathered, ((3, 3), (0, 0)))
    mixed_all = convolve(whole_pad, kernel, seq_len)
    grad_w_in = lax.dot_general(
        mixed_all, grad_rows, (((0,), (0,)), ((), ())), preferred_element_type=jnp.float32
    )
    offset = lax.axis_index(TP) * length
    padded = lax.dynamic_slice_in_dim(whole_pad, offset, length + 6, 0)
    grad_pad = with_halo(grad_mixed, ((TP, 0),), 3)
    grad_f = grad_mixed.astype(jnp.float32)
    grad_inputs = grad_f
    taps = []
    for tap in range(KW):
        grad_inputs = grad_inputs + kernel[tap] * grad_pad[6 - tap : 6 - tap + length].astype(
            jnp.float32
        )
        taps.append(jnp.sum(grad_f * padded[tap : tap + length].astype(jnp.float32), axis=0))
    grad_kernel = jnp.stack(taps)
    grad_kernel = over_copies(grad_kernel.astype(jnp.bfloat16), TP).astype(jnp.float32)
    grad_w_in, grad_w_out, grad_bias, grad_kernel = (
        lax.psum(grad_w_in.astype(jnp.bfloat16), "dp").astype(jnp.float32),
        lax.psum(grad_w_out.astype(jnp.bfloat16), "dp").astype(jnp.float32),
        lax.psum(grad_bias.astype(jnp.bfloat16), "dp").astype(jnp.float32),
        lax.psum(grad_kernel.astype(jnp.bfloat16), "dp").astype(jnp.float32),
    )
    return (grad_inputs.astype(jnp.bfloat16)[None], grad_w_in, grad_w_out, grad_bias, grad_kernel)


def solution(mesh):
    split = Mesh(mesh.devices.reshape(mesh.shape["dp"], 8, 2), ("dp", "tp_0", "tp_1"))
    in_specs = (
        P("dp", TP, None),
        P("dp", None, TP),
        P("dp", TP, None),
        P(None, TP),
        P(TP, None),
        P(),
    )
    out_specs = (P("dp", TP, None), P(None, TP), P(TP, None), P(TP), P())
    return jax.shard_map(
        shards, mesh=split, in_specs=in_specs, out_specs=out_specs, check_vma=False
    )
```

profile of v0, /device:TPU:2, one launch (start us, length us, event | category | flops | bytes accessed | tf_op | source)
XLA Modules:
  0.0 628.2 jit_solution(97258340310683543)
XLA Ops:
  7.2 0.0 copy-start
  7.2 0.0 copy-start.1
  7.2 0.0 all-gather.5.cloned.1.call-start
  7.2 0.7 all-gather.5.cloned.1.call-update
  7.9 0.0 reduce-scatter.3.cloned.1.call-start
  8.0 10.1 %fusion.52 = f32[3072,320]{0,1:T(8,128)} fusion(bf16[1,3072,320]{1,2,0:T(8,128)(2,1)} %param.7), kind=kLoop, calls=%fused_computation.64 | loop fusion | flops 61931520 | bytes 5898240 | tf_op jit(solution)/shard_map/jvp()/erfc | solution.py:45
  18.1 124.8 %all-gather.5.cloned.1.call-done = bf16[1,3072,1280]{2,1,0:T(8,128)(2,1)} async-done(((bf16[1,192,1280]{2,1,0:T(8,128)(2,1)}), bf16[1,3072,1280]{2,1,0:T(8,128)(2,1)}) %all-gather.5.cloned.1.call-update) | async-done | bytes 7864336 | tf_op jit(solution)/shard_map/all_gather | solution.py:61
  142.9 0.0 copy-done.1
  142.9 8.2 %fusion.87 = (bf16[320]{0:T(512)(128)(2,1)S(1)}, bf16[3072,320]{0,1:T(8,128)(2,1)S(1)}) fusion(f32[3072,320]{0,1:T(8,128)} %fusion.52, bf16[320,1280]{1,0:T(8,128)(2,1)} %param.10, bf16[1,3072,1280]{2,1,0:T(8,128)(2,1)} %all-gather.5.cloned.1.call-done, bf16[1,3072,320]{1,2,0:T(8,128)(2,1)S(1)} %copy-done.1), kind=kOutput, calls=%fused_computation.114 | convolution fusion | flops 2532310784 | bytes 16548480 | tf_op jit(solution)/shard_map/dot_general | solution.py:63
  151.1 0.0 copy-start.4
  151.1 1.3 copy-done.4
  152.4 0.0 copy-done
  152.4 6.4 %convolution_convert_fusion = bf16[3072,1280]{1,0:T(8,128)(2,1)} fusion(bf16[3072,320]{0,1:T(8,128)(2,1)S(1)} %get-tuple-element.27, bf16[1280,320]{0,1:T(8,128)(2,1)S(1)} %copy-done), kind=kOutput, calls=%fused_computation.9 | convolution fusion | flops 2520514560 | bytes 10649600 | tf_op jit(solution)/shard_map/dot_general | solution.py:74
  158.9 0.0 copy-start.3
  158.9 0.0 reduce-scatter.3.cloned.1.call-update
  158.9 0.0 all-gather.7.cloned.1.call-start
  158.9 0.7 all-gather.7.cloned.1.call-update
  159.6 0.0 reduce-scatter.5.cloned.1.call-start
  159.7 0.0 copy-done.3
  159.7 0.1 slice_reduce_fusion.6
  159.8 8.1 %fusion.58 = bf16[320,1280]{1,0:T(8,128)(2,1)} fusion(bf16[1,3072,1280]{2,1,0:T(8,128)(2,1)} %all-gather.5.cloned.1.call-done, f32[3072,320]{0,1:T(8,128)} %fusion.52, bf16[1,3072,320]{1,2,0:T(8,128)(2,1)S(1)} %copy-done.1), kind=kOutput, calls=%fused_computation.75 | convolution fusion | flops 2520924160 | bytes 14581760 | tf_op jit(solution)/shard_map/dot_general | solution.py:68
  167.9 78.8 %reduce-scatter.3.cloned.1.call-done = bf16[384,1280]{1,0:T(8,128)(2,1)} async-done(((bf16[3072,1280]{1,0:T(8,128)(2,1)}), bf16[384,1280]{1,0:T(8,128)(2,1)}) %reduce-scatter.3.cloned.1.call-update) | async-done | bytes 983056 | tf_op jit(solution)/shard_map/reduce_scatter | solution.py:14
  246.7 0.0 reduce-scatter.5.cloned.1.call-update
  246.8 0.2 all-reduce.5.cloned.1.call-start
  247.0 130.4 %all-gather.7.cloned.1.call-done = bf16[1,3072,1280]{2,1,0:T(8,128)(2,1)} async-done(((bf16[1,192,1280]{2,1,0:T(8,128)(2,1)}), bf16[1,3072,1280]{2,1,0:T(8,128)(2,1)}) %all-gather.7.cloned.1.call-update) | async-done | bytes 7864336 | tf_op jit(solution)/shard_map/all_gather | solution.py:80
  377.4 0.0 copy-start.2
  377.4 34.2 %fusion.55 = bf16[1280,320]{0,1:T(8,128)(2,1)} fusion(bf16[3072,320]{0,1:T(8,128)(2,1)} %copy-done.4, bf16[3072,1280]{1,0:T(8,128)(2,1)} %bitcast.127, f32[1280]{0:T(1024)S(1)} %get-tuple-element.17, f32[1280]{0:T(1024)S(1)} %get-tuple-element.18, f32[1280]{0:T(1024)S(1)} %get-tuple-element.13, f32[1280]{0:T(1024)S(1)} %get-tuple-element.14, ...), kind=kOutput, calls=%fused_computation.74 | convolution fusion | flops 2603499520 | bytes 10685440 | tf_op jit(solution)/shard_map/dot_general | solution.py:83
  411.6 0.0 all-reduce.5.cloned.1.call-update
  411.6 0.0 reduce-scatter.5.cloned.1.call-done
  411.7 0.0 copy-done.2
  411.7 4.0 fusion.76
  415.7 1.3 collective-permute-start
  417.0 6.1 collective-permute-start.1
  423.1 113.4 %all-reduce.5.cloned.1.call-done = (bf16[1280,320]{0,1:T(8,128)(2,1)}, bf16[320,1280]{1,0:T(8,128)(2,1)}) async-done(((bf16[1280,320]{0,1:T(8,128)(2,1)}, bf16[320,1280]{1,0:T(8,128)(2,1)}), (bf16[1280,320]{0,1:T(8,128)(2,1)}, bf16[320,1280]{1,0:T(8,128)(2,1)})) %all-reduce.5.cloned.1.call-update) | async-done | bytes 1638416 | tf_op jit(solution)/shard_map/psum | solution.py:100
  536.4 2.4 convert_element_type.141
  538.9 2.4 convert_element_type.144
  541.4 0.1 stack.39
  541.4 0.7 broadcast_in_dim.7
  542.2 8.6 %all-to-all-start = ((bf16[16,7,1280]{2,1,0:T(8,128)(2,1)}), bf16[16,7,1280]{2,1,0:T(8,128)(2,1)S(1)}, u32[]{:S(2)}, u32[]{:S(2)}) async-start(bf16[16,7,1280]{2,1,0:T(8,128)(2,1)} %broadcast_in_dim.7), calls=%async_computation.2 | async-start | bytes 655360 | tf_op jit(solution)/shard_map/all_to_all | solution.py:37
  550.8 0.0 collective-permute-done
  550.8 0.0 collective-permute-done.1
  550.8 1.7 fusion.82
  552.5 12.7 %all-to-all-done = bf16[16,7,1280]{2,1,0:T(8,128)(2,1)S(1)} async-done(((bf16[16,7,1280]{2,1,0:T(8,128)(2,1)}), bf16[16,7,1280]{2,1,0:T(8,128)(2,1)S(1)}, u32[]{:S(2)}, u32[]{:S(2)}) %all-to-all-start) | async-done | bytes 286752 | tf_op jit(solution)/shard_map/all_to_all | solution.py:37
  565.2 0.1 reduce_sum.95
  565.2 55.3 %all-reduce.1 = (bf16[320]{0:T(512)(128)(2,1)S(1)}, bf16[7,1280]{1,0:T(8,128)(2,1)S(1)}) all-reduce(bf16[320]{0:T(512)(128)(2,1)S(1)} %get-tuple-element.26, bf16[7,1280]{1,0:T(8,128)(2,1)S(1)} %reduce_sum.95), channel_id=1, replica_groups=mesh['dp'=16,'tp_0'=8,'tp_1'=2] {'dp'}, use_global_device_ids=true, to_apply=%region_5.6 | all-reduce | flops 9280 | bytes 37120 | tf_op jit(solution)/shard_map/psum | solution.py:102
  620.5 0.6 convert_element_type.145
  621.1 0.6 convert_element_type.153
  (8 shorter events, 0.1 us)
Async XLA Ops:
  7.2 145.3 %copy-start = (bf16[1280,320]{0,1:T(8,128)(2,1)S(1)}, bf16[1280,320]{0,1:T(8,128)(2,1)}, u32[]{:S(2)}) copy-start(bf16[1280,320]{0,1:T(8,128)(2,1)} %param.9) | copy-start | bytes 2457604
  7.2 135.7 %copy-start.1 = (bf16[1,3072,320]{1,2,0:T(8,128)(2,1)S(1)}, bf16[1,3072,320]{1,2,0:T(8,128)(2,1)}, u32[]{:S(2)}) copy-start(bf16[1,3072,320]{1,2,0:T(8,128)(2,1)} %param.7) | copy-start | bytes 5898244
  7.2 135.7 %all-gather.5.cloned.1.call-start = ((), (), s32[]{:S(2)}) async-start(), calls=%async_computation.5 | async-start | bytes 8355840 | tf_op jit(solution)/shard_map/all_gather | solution.py:61
  7.9 238.8 %reduce-scatter.3.cloned.1.call-start = ((), (), s32[]{:S(2)}) async-start(), calls=%async_computation.3 | async-start | bytes 8847360 | tf_op jit(solution)/shard_map/reduce_scatter | solution.py:14
  151.1 1.3 copy-start.4
  158.9 0.8 copy-start.3
  158.9 218.5 %all-gather.7.cloned.1.call-start = ((), (), s32[]{:S(2)}) async-start(), calls=%async_computation.6 | async-start | bytes 8355840 | tf_op jit(solution)/shard_map/all_gather | solution.py:80
  159.6 252.0 %reduce-scatter.5.cloned.1.call-start = ((), (), s32[]{:S(2)}) async-start(), calls=%async_computation.4 | async-start | bytes 1474560 | tf_op jit(solution)/shard_map/reduce_scatter | solution.py:14
  246.8 289.7 %all-reduce.5.cloned.1.call-start = ((), (), s32[]{:S(2)}) async-start(), calls=%async_computation.7 | async-start | bytes 3276800 | tf_op jit(solution)/shard_map/psum | solution.py:100
  377.4 34.3 %copy-start.2 = (bf16[1,192,1280]{2,1,0:T(8,128)(2,1)S(1)}, bf16[1,192,1280]{2,1,0:T(8,128)(2,1)}, u32[]{:S(2)}) copy-start(bf16[1,192,1280]{2,1,0:T(8,128)(2,1)} %param.8) | copy-start | bytes 1474564
  415.7 135.1 %collective-permute-start = (bf16[3,1280]{1,0:T(4,128)(2,1)S(1)}, bf16[3,1280]{1,0:T(4,128)(2,1)S(1)}, u32[]{:S(2)}, u32[]{:S(2)}) collective-permute-start(bf16[3,1280]{1,0:T(4,128)(2,1)S(1)} %get-tuple-element.24), channel_id=1, source_target_pairs={{1,0},{2,1},{3,2},{4,3},{5,4},{6,5},{7,6},{8,7},{9,8},{10,9},{11,1... | collective-permute-start | bytes 23048 | tf_op jit(solution)/shard_map/ppermute | solution.py:28
  417.0 133.8 %collective-permute-start.1 = (bf16[3,1280]{1,0:T(4,128)(2,1)S(1)}, bf16[3,1280]{1,0:T(4,128)(2,1)S(1)}, u32[]{:S(2)}, u32[]{:S(2)}) collective-permute-start(bf16[3,1280]{1,0:T(4,128)(2,1)S(1)} %get-tuple-element.25), channel_id=1, source_target_pairs={{0,1},{1,2},{2,3},{3,4},{4,5},{5,6},{6,7},{7,8},{8,9},{9,10},{10,1... | collective-permute-start | bytes 23048 | tf_op jit(solution)/shard_map/ppermute | solution.py:26
  542.2 23.0 %all-to-all-start = ((bf16[16,7,1280]{2,1,0:T(8,128)(2,1)}), bf16[16,7,1280]{2,1,0:T(8,128)(2,1)S(1)}, u32[]{:S(2)}, u32[]{:S(2)}) async-start(bf16[16,7,1280]{2,1,0:T(8,128)(2,1)} %broadcast_in_dim.7), calls=%async_computation.2 | async-start | bytes 655360 | tf_op jit(solution)/shard_map/all_to_all | solution.py:37
Sparse Core Ops, SparseCore 0:
  10.6 132.2 all-gather.4
  159.0 87.6 reduce-scatter.2
  249.3 127.9 all-gather.6
  379.7 23.0 reduce-scatter.4
  411.7 124.6 all-reduce.4
where the time goes:
time: 629 us; the launch traced here: 628 us
  waiting for transfers between devices  462 us (73%)
  matrix products  57 us (9%)
  blocking collectives  55.3 us (9%)
  other arithmetic  21.9 us (3%)
  starting transfers between devices  16.4 us (3%)
  between operations  13.9 us (2%)
    all_gather x1, waiting for transfers between devices, shards(): gathered = lax.all_gather(tokens, TP, axis=0, tiled=True)  130 us
    all_gather x1, waiting for transfers between devices, shards(): piece = lax.all_gather(grad_out, TP, axis=0, tiled=True)  125 us
    psum x1, waiting for transfers between devices, shards(): lax.psum(grad_w_in.astype(jnp.bfloat16), 'dp').astype(jnp.float32)  113 us
    reduce_scatter x2, waiting for transfers between devices, own_rows(): running = lax.psum_scatter(running, axis, scatter_dimension=0, tiled=True)  78.9 us
    psum x1, blocking collectives, shards(): lax.psum(grad_bias.astype(jnp.bfloat16), 'dp').astype(jnp.float32)  55.3 us
    dot_general x1, matrix products, shards(): lax.dot_general(mixed_all, grad_rows, (((0,), (0,)), ((), ())), preferred...  34.2 us
    all_to_all x1, waiting for transfers between devices, sent_to_all(): return lax.all_to_all(copies, axis, split_axis=0, concat_axis=0, tiled=True)  12.7 us
  transfers between devices with their start and end apart: 8, of which 5 were waited for; matrix products, arithmetic and copies ran while one was open for 10% of the time, Pallas kernels for 0%

commit v1 on v0

v1 whole, which is shorter than its diff:
```python
import functools

import jax
import jax.numpy as jnp
from jax import lax
from jax.experimental import pallas as pl
from jax.experimental.pallas import tpu as pltpu
from jax.sharding import PartitionSpec as P

KW = 7
D = 1280
H = 320
T = 192
SLOTS = 16
HR = 48
SR = 2 * HR
HOPS = SLOTS - 2
HALO = 16
MESH_ID = pl.DeviceIdType.MESH
F32 = jnp.float32
BF16 = jnp.bfloat16

LAG = 8
MIXED_AT = 4
GWO_AT = ((16, 17), (24, 25))
GWI_AT = ((22, 23), (30, 31))
DX_FROM = 26
RED_AT = ((26, 28, 33, 36, 39), (32, 34, 39, None, None))
STEPS = 3 * HOPS + 2


def dot_nt(a, b):
    return lax.dot_general(a, b, (((1,), (1,)), ((), ())), preferred_element_type=F32)


def gelu_parts(x):
    a = jnp.abs(x) * 0.7071067811865476
    t = 1.0 / (1.0 + 0.5 * a)
    p = 0.17087277
    for coef in (
        -0.82215223,
        1.48851587,
        -1.13520398,
        0.27886807,
        -0.18628806,
        0.09678418,
        0.37409196,
        1.00002368,
        -1.26551223,
    ):
        p = p * t + coef
    square = a * a
    tail = 0.5 * t * jnp.exp(p - square)
    cdf = jnp.where(x >= 0, 1.0 - tail, tail)
    slope = cdf + x * (0.3989422804014327 * jnp.exp(-square))
    return x * cdf, slope


def body(
    x_hbm, h_hbm, u_hbm, wi_hbm, wo_hbm, k_ref,
    gi_hbm, gwo_hbm, gwi_hbm, sm_ref,
    up, mx, dx, rr, hh, act, gh, wo, wi, gwo, gwi, actt, bias,
    cs, cr, ys, yr, xs, xr, fout,
    xb, xf, gf, gmb, gio, gib, sm, smc, smy, smx, smz, smf,
    z_send, z_recv, h_send, h_recv, h_load, w_send, w_recv, l_sem, o_sem,
    halo_send, halo_recv, red_send, red_recv, s_send, s_recv,
):
    dp, tp = lax.axis_index("dp"), lax.axis_index("tp")
    xl, y, c = dp // 8, (dp // 2) % 4, dp % 2
    z, xh = tp // 2, tp % 2
    me_x = xh * 2 + xl

    def z_dev(n):
        return (dp, (tp + 2 * n + 32) % 16)

    def y_dev(n):
        return (xl * 8 + ((y + n) % 4) * 2 + c, tp)

    core_dev = (dp + 1 - 2 * c, tp)
    xh_dev = (dp, tp + 1 - 2 * xh)
    xl_dev = (dp + 8 - 16 * xl, tp)
    xd_dev = (dp + 8 - 16 * xl, tp + 1 - 2 * xh)
    next_dev = (dp, (tp + 1) % 16)
    prev_dev = (dp, (tp + 15) % 16)

    def remote(src, dst, send, recv, device):
        return pltpu.make_async_remote_copy(
            src_ref=src, dst_ref=dst, send_sem=send, recv_sem=recv,
            device_id=device, device_id_type=MESH_ID,
        )

    def local_loads():
        copies = []
        n = 0
        for a in range(2):
            for half in range(2):
                copies.append(pltpu.make_async_copy(
                    u_hbm.at[0, pl.ds(half * 96 + a * HR, HR)], up.at[a, pl.ds(half * HR, HR)], l_sem.at[n]))
                n += 1
        copies.append(pltpu.make_async_copy(x_hbm.at[0], xb.at[pl.ds(HALO, T)], l_sem.at[n]))
        copies.append(pltpu.make_async_copy(wo_hbm, wo.at[0], l_sem.at[n + 1]))
        copies.append(pltpu.make_async_copy(wi_hbm, wi.at[0], l_sem.at[n + 2]))
        return copies

    def hidden_rows(slot, half, parity):
        s, a = slot // 2, slot % 2
        block = 2 * ((z + (s if half else 8 - s)) % 8) + parity
        start = pl.multiple_of(block * T + half * 96 + a * HR, 16)
        return h_hbm.at[0, pl.ds(start, HR)]

    def hidden_load(slot, half):
        return pltpu.make_async_copy(
            hidden_rows(slot, half, xh), hh.at[0, slot, pl.ds(half * HR, HR)], h_load.at[slot, half])

    def hidden_send(slot, half):
        return remote(
            hidden_rows(slot, half, 1 - xh), hh.at[1, slot, pl.ds(half * HR, HR)],
            h_send.at[slot, half], h_recv.at[slot, half], xh_dev)

    wo_copy = remote(wo_hbm, wo.at[1], w_send.at[0], w_recv.at[0], xh_dev)
    wi_copy = remote(wi_hbm, wi.at[1], w_send.at[1], w_recv.at[1], xh_dev)
    halo_copies = (
        remote(x_hbm.at[0, pl.ds(T - HALO, HALO)], xb.at[pl.ds(0, HALO)], halo_send.at[0], halo_recv.at[0], next_dev),
        remote(x_hbm.at[0, pl.ds(0, HALO)], xb.at[pl.ds(T + HALO, HALO)], halo_send.at[1], halo_recv.at[1], prev_dev),
    )

    def ring(phase, hop, half):
        rows = pl.ds(half * HR, HR)
        device = z_dev(-1 if half else 1)
        if phase == 0:
            src, dst = up.at[hop, rows], up.at[hop + 2, rows]
        elif phase == 1:
            src, dst = mx.at[hop, rows], mx.at[hop + 2, rows]
        else:
            src, dst = dx.at[hop + 2, rows], rr.at[hop, rows]
        return remote(src, dst, z_send.at[phase, hop, half], z_recv.at[phase, hop, half], device)

    locals_ = local_loads()
    for copy in locals_:
        copy.start()
    barrier = pltpu.get_barrier_semaphore()
    peers = [z_dev(n) for n in range(1, 8)] + [y_dev(n) for n in range(1, 4)]
    peers += [core_dev, xl_dev, xd_dev, next_dev, prev_dev]
    for peer in peers:
        pl.semaphore_signal(barrier, inc=1, device_id=peer, device_id_type=MESH_ID)
    pl.semaphore_wait(barrier, len(peers))

    for copy in halo_copies:
        copy.start()
    wo_copy.start()

    @pl.loop(0, SLOTS)
    def _(slot):
        for half in range(2):
            hidden_load(slot, half).start()

    bias[...] = jnp.zeros_like(bias)

    def red_core(m):
        return remote(cs.at[m, 1 - c], cr.at[m], red_send.at[m, 0], red_recv.at[m, 0], core_dev)

    def red_y(m, n):
        return remote(ys.at[m, (y + n) % 4], yr.at[m, n - 1], red_send.at[m, n], red_recv.at[m, n], y_dev(n))

    def red_x(m):
        return (
            remote(xs.at[m, 0], xr.at[m, me_x], red_send.at[m, 4], red_recv.at[m, 4], xl_dev),
            remote(xs.at[m, 1], xr.at[m, me_x], red_send.at[m, 5], red_recv.at[m, 5], xh_dev),
            remote(xs.at[m, 1], xr.at[m, me_x], red_send.at[m, 6], red_recv.at[m, 6], xd_dev),
        )

    def red_x_wait(m):
        for sem, src_x, device in (
            (4, xh * 2 + 1 - xl, xl_dev), (5, (1 - xh) * 2 + xl, xh_dev), (6, (1 - xh) * 2 + 1 - xl, xd_dev),
        ):
            remote(xs.at[m, 0], xr.at[m, src_x], red_send.at[m, sem], red_recv.at[m, sem], device).wait_recv()

    def ag_y(m, n, source):
        return remote(
            fout.at[m, c, source], fout.at[m, c, source], red_send.at[m, 6 + n], red_recv.at[m, 6 + n], y_dev(n))

    def ag_core(m, half):
        return remote(fout.at[m, half], fout.at[m, half], red_send.at[m, 10], red_recv.at[m, 10], core_dev)

    totals = (gwo, gwi)

    def reduce_stage(m, stage):
        total = totals[m]
        if stage == 0:
            for q in range(2):
                for half in range(2):
                    cs[m, half, q] = total[q, :, half * 640:(half + 1) * 640].astype(BF16)
            red_core(m).start()
        elif stage == 1:
            red_core(m).wait_recv()
            own_cols = pl.ds(pl.multiple_of(c * 640, 128), 640)
            for q in range(2):
                for part in range(4):
                    rows = slice(part * 80, part * 80 + 80)
                    ys[m, part, q] = (total[q, rows, own_cols] + cr[m, q, rows].astype(F32)).astype(BF16)
            for n in range(1, 4):
                red_y(m, n).start()
        elif stage == 2:
            for n in range(1, 4):
                red_y(m, n).wait_recv()
            for q in range(2):
                part = ys[m, y, q].astype(F32)
                for n in range(3):
                    part = part + yr[m, n, q].astype(F32)
                xs[m, q] = part.astype(BF16)
            for copy in red_x(m):
                copy.start()
        elif stage == 3:
            red_x_wait(m)
            xr[m, me_x] = xs[m, 0]
            part = xr[m, 0].astype(F32)
            for n in range(1, 4):
                part = part + xr[m, n].astype(F32)
            fout[m, c, y] = part.astype(BF16)
            for n in range(1, 4):
                ag_y(m, n, y).start()
        else:
            for n in range(1, 4):
                ag_y(m, n, (y + 4 - n) % 4).wait_recv()
            ag_core(m, c).start()

    def reduce_out(m):
        return pltpu.make_async_copy(fout.at[m], (gwo_hbm, gwi_hbm)[m], o_sem.at[m])

    def mixed_task():
        locals_[4].wait()
        for copy in halo_copies:
            copy.wait_recv()
        xf[pl.ds(HALO, T)] = xb[pl.ds(HALO, T)].astype(F32)
        xf[pl.ds(0, HALO)] = jnp.where(tp == 0, 0.0, xb[pl.ds(0, HALO)].astype(F32))
        xf[pl.ds(T + HALO, HALO)] = jnp.where(tp == 15, 0.0, xb[pl.ds(T + HALO, HALO)].astype(F32))

        @pl.loop(0, D // 128)
        def _(n):
            cols = pl.ds(pl.multiple_of(n * 128, 128), 128)
            taps = k_ref[:, cols]
            out = xf[HALO:HALO + T, cols]
            for tap in range(KW):
                out = out + taps[tap:tap + 1] * xf[HALO - 3 + tap:HALO - 3 + tap + T, cols]
            out = out.astype(BF16)
            for a in range(2):
                for half in range(2):
                    start = half * 96 + a * HR
                    mx[a, half * HR:(half + 1) * HR, cols] = out[start:start + HR]

    def hidden_task(slot):
        for half in range(2):
            hidden_load(slot, half).wait()
            hidden_send(slot, half).wait_recv()
        rows = up[slot]
        for q in range(2):
            back = dot_nt(rows, wo[q])
            value, slope = gelu_parts(hh[q, slot].astype(F32))
            grad = (slope * back).astype(BF16)
            act[q, slot] = value.astype(BF16)
            gh[q, slot] = grad
            bias[q] += jnp.sum(grad.astype(F32).reshape(SR // 8, 8, H), axis=0)

    def weight_task(left, right, total, q, part):
        eight = pl.ds(part * 8, 8)
        actt[...] = left[q, eight].reshape(8 * SR, H).T

        @pl.loop(0, D // 256)
        def _(n):
            cols = pl.ds(pl.multiple_of(n * 256, 256), 256)
            value = jnp.dot(
                actt[...], right[eight, :, cols].reshape(8 * SR, 256), preferred_element_type=F32)
            if part == 0:
                total[q, :, cols] = value
            else:
                total[q, :, cols] += value

    def dx_task(slot):
        g0, g1 = gh[0, slot], gh[1, slot]
        for n in range(D // 256):
            rows = slice(n * 256, n * 256 + 256)
            dx[slot, :, rows] = (dot_nt(g0, wi[0, rows]) + dot_nt(g1, wi[1, rows])).astype(BF16)

    for n in range(4):
        locals_[n].wait()

    def at(step, i):
        return pl.when(i == step)

    def step(i, carry):
        @pl.when((i >= 2) & (i < 16))
        def _():
            for half in range(2):
                ring(0, i - 2, half).wait_recv()

        @pl.when(i < HOPS)
        def _():
            for half in range(2):
                ring(0, i, half).start()

        @pl.when((i >= 16) & (i < 30))
        def _():
            for half in range(2):
                ring(1, i - 16, half).wait_recv()

        @pl.when((i >= 14) & (i < 28))
        def _():
            for half in range(2):
                ring(1, i - 14, half).start()

        @pl.when((i >= 30) & (i < 42))
        def _():
            for half in range(2):
                ring(2, i - 30, half).wait_recv()
            slot = i - 26
            dx[slot] = (dx[slot].astype(F32) + rr[i - 30].astype(F32)).astype(BF16)

        @pl.when((i >= 28) & (i < 42))
        def _():
            for half in range(2):
                ring(2, i - 28, half).start()

        @pl.when(i < 8)
        def _():
            for j in range(2):
                for half in range(2):
                    hidden_send(2 * i + j, half).start()

        @at(8, i)
        def _():
            wi_copy.start()
            locals_[5].wait()
            wo_copy.wait_recv()

        at(MIXED_AT, i)(mixed_task)

        @pl.when((i >= LAG) & (i < LAG + SLOTS))
        def _():
            hidden_task(i - LAG)

        for part in range(2):
            for q in range(2):
                at(GWO_AT[part][q], i)(functools.partial(weight_task, act, up, gwo, q, part))
                at(GWI_AT[part][q], i)(functools.partial(weight_task, gh, mx, gwi, q, part))

        @at(DX_FROM, i)
        def _():
            locals_[6].wait()
            wi_copy.wait_recv()

        @pl.when((i >= DX_FROM) & (i < DX_FROM + SLOTS))
        def _():
            dx_task((i - DX_FROM + 2) % SLOTS)

        for m in range(2):
            for stage in range(5):
                if RED_AT[m][stage] is not None:
                    at(RED_AT[m][stage], i)(functools.partial(reduce_stage, m, stage))
        return carry

    lax.fori_loop(0, STEPS - 2, step, 0)

    for a in range(2):
        for half in range(2):
            ring(2, HOPS - 2 + a, half).wait_recv()
        done = up[a].astype(F32) + (dx[a].astype(F32) + rr[HOPS - 2 + a].astype(F32))
        done = done.astype(BF16)
        for half in range(2):
            start = half * 96 + a * HR
            gmb[start:start + HR] = done[half * HR:(half + 1) * HR]
            gf[HALO + start:HALO + start + HR] = done[half * HR:(half + 1) * HR].astype(F32)
    edge_copies = (
        remote(gmb.at[pl.ds(T - HALO, HALO)], gib.at[0], halo_send.at[2], halo_recv.at[2], next_dev),
        remote(gmb.at[pl.ds(0, HALO)], gib.at[1], halo_send.at[3], halo_recv.at[3], prev_dev),
    )
    for copy in edge_copies:
        copy.start()

    reduce_stage(1, 3)

    sm[7:8] = jnp.zeros((1, D), F32)
    b0 = jnp.sum(bias[0], axis=0, keepdims=True)
    b1 = jnp.sum(bias[1], axis=0, keepdims=True)
    sm[7:8, 0:H] = jnp.where(xh == 0, b0, b1)
    sm[7:8, 384:384 + H] = jnp.where(xh == 0, b1, b0)

    @pl.loop(0, D // 128)
    def _(n):
        cols = pl.ds(pl.multiple_of(n * 128, 128), 128)
        grad = gf[HALO:HALO + T, cols]
        for tap in range(KW):
            product = grad * xf[HALO - 3 + tap:HALO - 3 + tap + T, cols]
            sm[tap:tap + 1, cols] = jnp.sum(product, axis=0, keepdims=True)

    def sm_core():
        return remote(sm, smc, s_send.at[0], s_recv.at[0], core_dev)

    def sm_y(n, source):
        return remote(smy.at[source], smy.at[source], s_send.at[n], s_recv.at[n], y_dev(n))

    def sm_x(n, source, device):
        return remote(smx.at[source], smx.at[source], s_send.at[4 + n], s_recv.at[4 + n], device)

    def sm_z(n, source):
        return remote(smz.at[source], smz.at[source], s_send.at[6 + n], s_recv.at[6 + n], z_dev(n))

    def sm_last(half):
        return remote(smf.at[half], smf.at[half], s_send.at[14], s_recv.at[14], core_dev)

    sm_core().start()

    reduce_stage(1, 4)

    sm_core().wait_recv()
    own_cols = pl.ds(pl.multiple_of(c * 640, 128), 640)
    smy[y] = sm[:, own_cols] + smc[:, own_cols]
    for n in range(1, 4):
        sm_y(n, y).start()

    for copy in edge_copies:
        copy.wait_recv()
    gf[pl.ds(0, HALO)] = jnp.where(tp == 0, 0.0, gib[0].astype(F32))
    gf[pl.ds(T + HALO, HALO)] = jnp.where(tp == 15, 0.0, gib[1].astype(F32))

    for n in range(1, 4):
        sm_y(n, (y + 4 - n) % 4).wait_recv()
    smx[me_x] = (smy[0] + smy[1]) + (smy[2] + smy[3])
    x_devices = (xl_dev, xh_dev, xd_dev)
    for n in range(3):
        sm_x(n, me_x, x_devices[n]).start()

    @pl.loop(0, D // 128)
    def _(n):
        cols = pl.ds(pl.multiple_of(n * 128, 128), 128)
        taps = k_ref[:, cols]
        out = gf[HALO:HALO + T, cols]
        for tap in range(KW):
            out = out + taps[tap:tap + 1] * gf[HALO + 3 - tap:HALO + 3 - tap + T, cols]
        gio[:, cols] = out.astype(BF16)

    gi_out = pltpu.make_async_copy(gio, gi_hbm.at[0], o_sem.at[2])
    gi_out.start()

    for n, source in enumerate((xh * 2 + 1 - xl, (1 - xh) * 2 + xl, (1 - xh) * 2 + 1 - xl)):
        sm_x(n, source, x_devices[n]).wait_recv()
    summed = (smx[0] + smx[1]) + (smx[2] + smx[3])
    smz[z] = summed
    for n in range(1, 8):
        sm_z(n, z).start()

    ag_core(1, 1 - c).wait_recv()
    ag_core(0, 1 - c).wait_recv()
    for m in range(2):
        reduce_out(m).start()

    for n in range(1, 8):
        sm_z(n, (z + 8 - n) % 8).wait_recv()
    whole = smz[0]
    for n in range(1, 8):
        whole = whole + smz[n]
    row = lax.broadcasted_iota(jnp.int32, (8, 640), 0)
    smf[c] = jnp.where(row == 7, smz[z], whole)
    sm_last(c).start()

    @pl.loop(0, HOPS)
    def _(hop):
        for phase in range(3):
            for half in range(2):
                ring(phase, hop, half).wait_send()

    @pl.loop(0, SLOTS)
    def _(slot):
        for half in range(2):
            hidden_send(slot, half).wait_send()

    wo_copy.wait_send()
    wi_copy.wait_send()
    for copy in halo_copies + edge_copies:
        copy.wait_send()
    for m in range(2):
        red_core(m).wait_send()
        for n in range(1, 4):
            red_y(m, n).wait_send()
            ag_y(m, n, y).wait_send()
        for copy in red_x(m):
            copy.wait_send()
        ag_core(m, c).wait_send()
    sm_core().wait_send()
    for n in range(1, 4):
        sm_y(n, y).wait_send()
    for n in range(3):
        sm_x(n, me_x, x_devices[n]).wait_send()
    for n in range(1, 8):
        sm_z(n, z).wait_send()
    gi_out.wait()
    for m in range(2):
        reduce_out(m).wait()
    sm_last(1 - c).wait_recv()
    sm_ref[...] = smf[...]
    sm_last(c).wait_send()


def shards(inputs, saved_hidden, upstream, w_in, w_out, kernel):
    anyspace = pl.BlockSpec(memory_space=pl.ANY)
    vmem = pl.BlockSpec(memory_space=pltpu.VMEM)
    dma = pltpu.SemaphoreType.DMA
    grad_inputs, gwo, gwi, small = pl.pallas_call(
        body,
        out_shape=(
            jax.ShapeDtypeStruct((1, T, D), BF16),
            jax.ShapeDtypeStruct((2, 4, 80, 640), BF16),
            jax.ShapeDtypeStruct((2, 4, 80, 640), BF16),
            jax.ShapeDtypeStruct((2, 8, 640), F32),
        ),
        in_specs=[anyspace] * 5 + [vmem],
        out_specs=(anyspace, anyspace, anyspace, vmem),
        scratch_shapes=[
            pltpu.VMEM((SLOTS, SR, D), BF16),
            pltpu.VMEM((SLOTS, SR, D), BF16),
            pltpu.VMEM((SLOTS, SR, D), BF16),
            pltpu.VMEM((HOPS, SR, D), BF16),
            pltpu.VMEM((2, SLOTS, SR, H), BF16),
            pltpu.VMEM((2, SLOTS, SR, H), BF16),
            pltpu.VMEM((2, SLOTS, SR, H), BF16),
            pltpu.VMEM((2, H, D), BF16),
            pltpu.VMEM((2, D, H), BF16),
            pltpu.VMEM((2, H, D), F32),
            pltpu.VMEM((2, H, D), F32),
            pltpu.VMEM((H, 8 * SR), BF16),
            pltpu.VMEM((2, 8, H), F32),
            pltpu.VMEM((2, 2, 2, H, 640), BF16),
            pltpu.VMEM((2, 2, H, 640), BF16),
            pltpu.VMEM((2, 4, 2, 80, 640), BF16),
            pltpu.VMEM((2, 3, 2, 80, 640), BF16),
            pltpu.VMEM((2, 2, 80, 640), BF16),
            pltpu.VMEM((2, 4, 80, 640), BF16),
            pltpu.VMEM((2, 2, 4, 80, 640), BF16),
            pltpu.VMEM((T + 2 * HALO, D), BF16),
            pltpu.VMEM((T + 2 * HALO, D), F32),
            pltpu.VMEM((T + 2 * HALO, D), F32),
            pltpu.VMEM((T, D), BF16),
            pltpu.VMEM((T, D), BF16),
            pltpu.VMEM((2, HALO, D), BF16),
            pltpu.VMEM((8, D), F32),
            pltpu.VMEM((8, D), F32),
            pltpu.VMEM((4, 8, 640), F32),
            pltpu.VMEM((4, 8, 640), F32),
            pltpu.VMEM((8, 8, 640), F32),
            pltpu.VMEM((2, 8, 640), F32),
            dma((3, HOPS, 2)), dma((3, HOPS, 2)),
            dma((SLOTS, 2)), dma((SLOTS, 2)), dma((SLOTS, 2)),
            dma((2,)), dma((2,)), dma((7,)), dma((3,)),
            dma((4,)), dma((4,)),
            dma((2, 11)), dma((2, 11)),
            dma((15,)), dma((15,)),
        ],
        compiler_params=pltpu.CompilerParams(
            collective_id=0, has_side_effects=True, vmem_limit_bytes=64 * 1024 * 1024 - 65536),
        name="step",
    )(inputs, saved_hidden, upstream, w_in, w_out, kernel)
    grad_w_out = jnp.concatenate([gwo[0].reshape(H, 640), gwo[1].reshape(H, 640)], axis=1).astype(F32)
    grad_w_in = gwi.reshape(2, H, 640).transpose(0, 2, 1).reshape(D, H).astype(F32)
    small = jnp.concatenate([small[0], small[1]], axis=1)
    parity = lax.axis_index("tp") % 2
    grad_bias = jnp.where(parity == 0, small[7, :H], small[7, 384:384 + H])
    return grad_inputs, grad_w_in, grad_w_out, grad_bias, small[:KW]


def solution(mesh):
    in_specs = (
        P("dp", "tp", None), P("dp", None, "tp"), P("dp", "tp", None), P(None, "tp"), P("tp", None), P())
    out_specs = (P("dp", "tp", None), P(None, "tp"), P("tp", None), P("tp"), P())
    return jax.shard_map(shards, mesh=mesh, in_specs=in_specs, out_specs=out_specs, check_vma=False)
```

time: 629 us -> 166 us (0.26)
  waiting for transfers between devices: 462 us -> 0 us
  Pallas kernels: 0 us -> 152 us
  matrix products: 57 us -> 0 us
  blocking collectives: 55.3 us -> 0 us
  other arithmetic: 21.9 us -> 3.75 us
  starting transfers between devices: 16.4 us -> 0 us
  between operations: 13.9 us -> 0.68 us
    all_gather x2 -> x0, waiting for transfers between devices: 255 us -> none  [the longest x1 130 us: shards(): gathered = lax.all_gather(tokens, TP, axis=0, tiled=True)]
    pallas_call x0 -> x1, Pallas kernels: none -> 152 us  [shards(): pl.pallas_call(body, out_shape=(jax.ShapeDtypeStruct((1, T, D), BF16), ja...]
    psum x1 -> x0, waiting for transfers between devices: 113 us -> none  [shards(): lax.psum(grad_w_in.astype(jnp.bfloat16), 'dp').astype(jnp.float32)]
    reduce_scatter x2 -> x0, waiting for transfers between devices: 78.9 us -> none  [own_rows(): running = lax.psum_scatter(running, axis, scatter_dimension=0, tiled=True)]
    dot_general x4 -> x0, matrix products: 57 us -> none  [the longest x1 34.2 us: shards(): lax.dot_general(mixed_all, grad_rows, (((0,), (0,)), ((), ())), preferred...]
    psum x1 -> x0, blocking collectives: 55.3 us -> none  [shards(): lax.psum(grad_bias.astype(jnp.bfloat16), 'dp').astype(jnp.float32)]
    all_to_all x1 -> x0, waiting for transfers between devices: 12.7 us -> none  [sent_to_all(): return lax.all_to_all(copies, axis, split_axis=0, concat_axis=0, tiled=True)]
    another operation x1 -> x0, other arithmetic: 10.1 us -> none  [gelu_exact(): return jax.nn.gelu(value, approximate=False)]
  transfers between devices with their start and end apart: 8 -> 0, of which waited for: 5 -> 0; matrix products, arithmetic and copies ran while one was open for 10% -> 0% of each run, Pallas kernels for 0% -> 0%
where the time goes in v1:
time: 166 us; the launch traced here: 164 us
  Pallas kernels  152 us (92%)
  local copies, waits for them, and re-layouts  7.71 us (5%)
  other arithmetic  3.75 us (2%)
    pallas_call x1, Pallas kernels, shards(): pl.pallas_call(body, out_shape=(jax.ShapeDtypeStruct((1, T, D), BF16), ja...  152 us
    unnamed x11, local copies, waits for them, and re-layouts  6.35 us

profile of v1, /device:TPU:2, one launch (start us, length us, event | category | flops | bytes accessed | tf_op | source)
XLA Modules:
  0.0 163.7 jit_solution(6339487044455689169)
XLA Ops:
  0.6 0.0 copy-start
  0.6 4.2 %copy.11.h_hbm = bf16[1,3072,320]{2,1,0:T(8,128)(2,1)} copy(bf16[1,3072,320]{1,2,0:T(8,128)(2,1)} %param.7) | data formatting | bytes 3932160 | tf_op args[1]
  4.8 0.0 copy-done
  4.8 1.3 copy.12.wi_hbm
  6.1 151.6 %step.1 = (bf16[1,192,1280]{2,1,0:T(8,128)(2,1)}, bf16[2,4,80,640]{3,2,1,0:T(8,128)(2,1)}, bf16[2,4,80,640]{3,2,1,0:T(8,128)(2,1)}, f32[2,8,640]{2,1,0:T(8,128)}) custom-call(bf16[1,192,1280]{2,1,0:T(8,128)(2,1)} %x_hbm.1, bf16[1,3072,320]{2,1,0:T(8,128)(2,1)} %copy.11.h_hbm, bf16[1,192,1280]{2,1,0:T(8,128)(2,1)} %u_hbm.1, bf16[1280,320]{1,0:T(8,128)(2,1)} %copy.12.wi_hbm, ...), custom_call_target="tpu_custom_call" | custom-call | tf_op jit(solution)/shard_map/step/pallas_call | solution.py:507
  157.7 1.3 convert_bitcast_fusion
  159.0 0.0 copy-start.1
  159.0 1.3 copy.14
  160.3 0.1 copy-done.1
  160.4 0.1 fusion.1
  160.4 0.0 copy-start.3
  160.4 0.0 copy-start.2
  160.4 1.3 maximum_convert_fusion
  161.7 0.0 copy-done.3
  161.7 0.6 fusion
  162.3 0.6 pad_maximum_fusion
  162.9 0.0 copy-done.2
  162.9 0.8 copy.16
  (1 shorter events, 0.0 us)
Async XLA Ops:
  0.6 4.2 %copy-start = (bf16[1280,320]{0,1:T(8,128)(2,1)S(1)}, bf16[1280,320]{0,1:T(8,128)(2,1)}, u32[]{:S(2)}) copy-start(bf16[1280,320]{0,1:T(8,128)(2,1)} %param.9) | copy-start | bytes 2457604
  159.0 1.4 copy-start.1
  160.4 1.3 copy-start.3
  160.4 2.5 %copy-start.2 = (bf16[1,192,1280]{2,1,0:T(8,128)(2,1)S(1)}, bf16[1,192,1280]{2,1,0:T(8,128)(2,1)}, u32[]{:S(2)}) copy-start(bf16[1,192,1280]{2,1,0:T(8,128)(2,1)} %get-tuple-element.22) | copy-start | bytes 1474564

commit v2 on v1

--- a/solution.py
+++ b/solution.py
@@ -25,7 +25,7 @@
 GWO_AT = ((16, 17), (24, 25))
 GWI_AT = ((22, 23), (30, 31))
 DX_FROM = 26
-RED_AT = ((26, 28, 33, 36, 39), (32, 34, 39, None, None))
+RED_AT = ((26, 28, 33, 36, 39), (31, 32, 36, 39, None))
 STEPS = 3 * HOPS + 2
 
 
@@ -59,9 +59,9 @@
 def body(
     x_hbm, h_hbm, u_hbm, wi_hbm, wo_hbm, k_ref,
     gi_hbm, gwo_hbm, gwi_hbm, sm_ref,
-    up, mx, dx, rr, hh, act, gh, wo, wi, gwo, gwi, actt, bias,
+    up, mx, dx, rr, ht, hrow, hh, act, gh, wo, wi, gwo, gwi, actt, bias,
     cs, cr, ys, yr, xs, xr, fout,
-    xb, xf, gf, gmb, gio, gib, sm, smc, smy, smx, smz, smf,
+    xb, xf, gf, gmb, gio, gib, sm, sms, smc, smy, smx, smz,
     z_send, z_recv, h_send, h_recv, h_load, w_send, w_recv, l_sem, o_sem,
     halo_send, halo_recv, red_send, red_recv, s_send, s_recv,
 ):
@@ -102,19 +102,23 @@
         copies.append(pltpu.make_async_copy(wi_hbm, wi.at[0], l_sem.at[n + 2]))
         return copies
 
+    def hidden_chunk(n):
+        return (z + 8 + ((n + 1) // 2) * (1 - 2 * (n % 2))) % 8
+
+    def hidden_load(n):
+        chunk = hidden_chunk(n)
+        cols = pl.ds(pl.multiple_of(chunk * 2 * T, 128), 2 * T)
+        return pltpu.make_async_copy(h_hbm.at[0, :, cols], ht.at[chunk], h_load.at[n])
+
     def hidden_rows(slot, half, parity):
         s, a = slot // 2, slot % 2
-        block = 2 * ((z + (s if half else 8 - s)) % 8) + parity
-        start = pl.multiple_of(block * T + half * 96 + a * HR, 16)
-        return h_hbm.at[0, pl.ds(start, HR)]
-
-    def hidden_load(slot, half):
-        return pltpu.make_async_copy(
-            hidden_rows(slot, half, xh), hh.at[0, slot, pl.ds(half * HR, HR)], h_load.at[slot, half])
+        chunk = (z + (s if half else 8 - s)) % 8
+        return chunk, pl.ds(pl.multiple_of(parity * T + half * 96 + a * HR, 16), HR)
 
     def hidden_send(slot, half):
+        chunk, rows = hidden_rows(slot, half, 1 - xh)
         return remote(
-            hidden_rows(slot, half, 1 - xh), hh.at[1, slot, pl.ds(half * HR, HR)],
+            hrow.at[chunk, rows], hh.at[slot, pl.ds(half * HR, HR)],
             h_send.at[slot, half], h_recv.at[slot, half], xh_dev)
 
     wo_copy = remote(wo_hbm, wo.at[1], w_send.at[0], w_recv.at[0], xh_dev)
@@ -138,9 +142,11 @@
     locals_ = local_loads()
     for copy in locals_:
         copy.start()
+    for n in range(8):
+        hidden_load(n).start()
     barrier = pltpu.get_barrier_semaphore()
-    peers = [z_dev(n) for n in range(1, 8)] + [y_dev(n) for n in range(1, 4)]
-    peers += [core_dev, xl_dev, xd_dev, next_dev, prev_dev]
+    peers = [z_dev(1), z_dev(-1)] + [y_dev(n) for n in range(1, 4)]
+    peers += [core_dev, xl_dev, xh_dev, xd_dev, next_dev, prev_dev]
     for peer in peers:
         pl.semaphore_signal(barrier, inc=1, device_id=peer, device_id_type=MESH_ID)
     pl.semaphore_wait(barrier, len(peers))
@@ -148,11 +154,6 @@
     for copy in halo_copies:
         copy.start()
     wo_copy.start()
-
-    @pl.loop(0, SLOTS)
-    def _(slot):
-        for half in range(2):
-            hidden_load(slot, half).start()
 
     bias[...] = jnp.zeros_like(bias)
 
@@ -177,7 +178,7 @@
 
     def ag_y(m, n, source):
         return remote(
-            fout.at[m, c, source], fout.at[m, c, source], red_send.at[m, 6 + n], red_recv.at[m, 6 + n], y_dev(n))
+            fout.at[m, c, pl.ds(source * 80, 80)], fout.at[m, c, pl.ds(source * 80, 80)], red_send.at[m, 6 + n], red_recv.at[m, 6 + n], y_dev(n))
 
     def ag_core(m, half):
         return remote(fout.at[m, half], fout.at[m, half], red_send.at[m, 10], red_recv.at[m, 10], core_dev)
@@ -216,7 +217,7 @@
             part = xr[m, 0].astype(F32)
             for n in range(1, 4):
                 part = part + xr[m, n].astype(F32)
-            fout[m, c, y] = part.astype(BF16)
+            fout[m, c, pl.ds(y * 80, 80)] = part.astype(BF16)
             for n in range(1, 4):
                 ag_y(m, n, y).start()
         else:
@@ -224,8 +225,9 @@
                 ag_y(m, n, (y + 4 - n) % 4).wait_recv()
             ag_core(m, c).start()
 
-    def reduce_out(m):
-        return pltpu.make_async_copy(fout.at[m], (gwo_hbm, gwi_hbm)[m], o_sem.at[m])
+    def reduce_out(m, half):
+        cols = pl.ds(half * 640, 640)
+        return pltpu.make_async_copy(fout.at[m, half], (gwo_hbm, gwi_hbm)[m].at[:, cols], o_sem.at[m, half])
 
     def mixed_task():
         locals_[4].wait()
@@ -250,12 +252,16 @@
 
     def hidden_task(slot):
         for half in range(2):
-            hidden_load(slot, half).wait()
             hidden_send(slot, half).wait_recv()
         rows = up[slot]
+        own = []
+        for half in range(2):
+            chunk, where = hidden_rows(slot, half, xh)
+            own.append(hrow[chunk, where])
+        own = jnp.concatenate(own, axis=0)
         for q in range(2):
             back = dot_nt(rows, wo[q])
-            value, slope = gelu_parts(hh[q, slot].astype(F32))
+            value, slope = gelu_parts((hh[slot] if q else own).astype(F32))
             grad = (slope * back).astype(BF16)
             act[q, slot] = value.astype(BF16)
             gh[q, slot] = grad
@@ -279,7 +285,10 @@
         g0, g1 = gh[0, slot], gh[1, slot]
         for n in range(D // 256):
             rows = slice(n * 256, n * 256 + 256)
-            dx[slot, :, rows] = (dot_nt(g0, wi[0, rows]) + dot_nt(g1, wi[1, rows])).astype(BF16)
+            dx[slot, :, rows] = (
+                jnp.dot(g0, wi[0, :, rows], preferred_element_type=F32)
+                + jnp.dot(g1, wi[1, :, rows], preferred_element_type=F32)
+            ).astype(BF16)
 
     for n in range(4):
         locals_[n].wait()
@@ -322,9 +331,22 @@
 
         @pl.when(i < 8)
         def _():
+            hidden_load(i).wait()
+            chunk = hidden_chunk(i)
+            hrow[chunk] = ht[chunk].T
+
+        @pl.when((i < 8) & (i % 2 == 0))
+        def _():
             for j in range(2):
                 for half in range(2):
-                    hidden_send(2 * i + j, half).start()
+                    hidden_send(i + j, half).start()
+
+        @at(7, i)
+        def _():
+            @pl.loop(8, SLOTS)
+            def _(slot):
+                for half in range(2):
+                    hidden_send(slot, half).start()
 
         @at(8, i)
         def _():
@@ -360,6 +382,15 @@
 
     lax.fori_loop(0, STEPS - 2, step, 0)
 
+    edge_copies = (
+        remote(gmb.at[pl.ds(T - HALO, HALO)], gib.at[0], halo_send.at[2], halo_recv.at[2], next_dev),
+        remote(gmb.at[pl.ds(0, HALO)], gib.at[1], halo_send.at[3], halo_recv.at[3], prev_dev),
+    )
+    sm[7:8] = jnp.zeros((1, D), F32)
+    b0 = jnp.sum(bias[0], axis=0, keepdims=True)
+    b1 = jnp.sum(bias[1], axis=0, keepdims=True)
+    sm[7:8, 0:H] = jnp.where(xh == 0, b0, b1)
+    sm[7:8, 384:384 + H] = jnp.where(xh == 0, b1, b0)
     for a in range(2):
         for half in range(2):
             ring(2, HOPS - 2 + a, half).wait_recv()
@@ -369,31 +400,30 @@
             start = half * 96 + a * HR
             gmb[start:start + HR] = done[half * HR:(half + 1) * HR]
             gf[HALO + start:HALO + start + HR] = done[half * HR:(half + 1) * HR].astype(F32)
-    edge_copies = (
-        remote(gmb.at[pl.ds(T - HALO, HALO)], gib.at[0], halo_send.at[2], halo_recv.at[2], next_dev),
-        remote(gmb.at[pl.ds(0, HALO)], gib.at[1], halo_send.at[3], halo_recv.at[3], prev_dev),
-    )
-    for copy in edge_copies:
-        copy.start()
-
-    reduce_stage(1, 3)
-
-    sm[7:8] = jnp.zeros((1, D), F32)
-    b0 = jnp.sum(bias[0], axis=0, keepdims=True)
-    b1 = jnp.sum(bias[1], axis=0, keepdims=True)
-    sm[7:8, 0:H] = jnp.where(xh == 0, b0, b1)
-    sm[7:8, 384:384 + H] = jnp.where(xh == 0, b1, b0)
-
-    @pl.loop(0, D // 128)
-    def _(n):
-        cols = pl.ds(pl.multiple_of(n * 128, 128), 128)
-        grad = gf[HALO:HALO + T, cols]
-        for tap in range(KW):
-            product = grad * xf[HALO - 3 + tap:HALO - 3 + tap + T, cols]
-            sm[tap:tap + 1, cols] = jnp.sum(product, axis=0, keepdims=True)
+        edge_copies[1 - a].start()
+
+        @pl.loop(0, D // 128)
+        def _(n):
+            cols = pl.ds(pl.multiple_of(n * 128, 128), 128)
+            for tap in range(KW):
+                added = jnp.zeros((1, 128), F32)
+                for half in range(2):
+                    start = HALO + half * 96 + a * HR
+                    product = gf[start:start + HR, cols] * xf[start - 3 + tap:start - 3 + tap + HR, cols]
+                    added = added + jnp.sum(product, axis=0, keepdims=True)
+                if a == 0:
+                    sm[tap:tap + 1, cols] = added
+                else:
+                    sm[tap:tap + 1, cols] += added
+
+        if a == 0:
+            reduce_stage(1, 4)
+            ag_core(0, 1 - c).wait_recv()
+            for half in range(2):
+                reduce_out(0, half).start()
 
     def sm_core():
-        return remote(sm, smc, s_send.at[0], s_recv.at[0], core_dev)
+        return remote(sms, smc, s_send.at[0], s_recv.at[0], core_dev)
 
     def sm_y(n, source):
         return remote(smy.at[source], smy.at[source], s_send.at[n], s_recv.at[n], y_dev(n))
@@ -404,30 +434,37 @@
     def sm_z(n, source):
         return remote(smz.at[source], smz.at[source], s_send.at[6 + n], s_recv.at[6 + n], z_dev(n))
 
-    def sm_last(half):
-        return remote(smf.at[half], smf.at[half], s_send.at[14], s_recv.at[14], core_dev)
-
+    def added_up(ref, count):
+        total = ref[0].astype(F32)
+        for n in range(1, count):
+            total = total + ref[n].astype(F32)
+        return total
+
+    sms[0:8] = sm[:, 0:640].astype(BF16)
+    sms[8:16] = sm[:, 640:1280].astype(BF16)
     sm_core().start()
-
-    reduce_stage(1, 4)
-
     sm_core().wait_recv()
-    own_cols = pl.ds(pl.multiple_of(c * 640, 128), 640)
-    smy[y] = sm[:, own_cols] + smc[:, own_cols]
+    smy[y] = (sms[...].astype(F32) + smc[...].astype(F32)).astype(BF16)
     for n in range(1, 4):
         sm_y(n, y).start()
-
     for copy in edge_copies:
         copy.wait_recv()
     gf[pl.ds(0, HALO)] = jnp.where(tp == 0, 0.0, gib[0].astype(F32))
     gf[pl.ds(T + HALO, HALO)] = jnp.where(tp == 15, 0.0, gib[1].astype(F32))
-
     for n in range(1, 4):
         sm_y(n, (y + 4 - n) % 4).wait_recv()
-    smx[me_x] = (smy[0] + smy[1]) + (smy[2] + smy[3])
+    smx[me_x] = added_up(smy, 4).astype(BF16)
     x_devices = (xl_dev, xh_dev, xd_dev)
     for n in range(3):
         sm_x(n, me_x, x_devices[n]).start()
+    ag_core(1, 1 - c).wait_recv()
+    for half in range(2):
+        reduce_out(1, half).start()
+    for n, source in enumerate((xh * 2 + 1 - xl, (1 - xh) * 2 + xl, (1 - xh) * 2 + 1 - xl)):
+        sm_x(n, source, x_devices[n]).wait_recv()
+    smz[z] = added_up(smx, 4).astype(BF16)
+    for n in range(1, 8):
+        sm_z(n, z).start()
 
     @pl.loop(0, D // 128)
     def _(n):
@@ -438,29 +475,8 @@
             out = out + taps[tap:tap + 1] * gf[HALO + 3 - tap:HALO + 3 - tap + T, cols]
         gio[:, cols] = out.astype(BF16)
 
-    gi_out = pltpu.make_async_copy(gio, gi_hbm.at[0], o_sem.at[2])
+    gi_out = pltpu.make_async_copy(gio, gi_hbm.at[0], o_sem.at[2, 0])
     gi_out.start()
-
-    for n, source in enumerate((xh * 2 + 1 - xl, (1 - xh) * 2 + xl, (1 - xh) * 2 + 1 - xl)):
-        sm_x(n, source, x_devices[n]).wait_recv()
-    summed = (smx[0] + smx[1]) + (smx[2] + smx[3])
-    smz[z] = summed
-    for n in range(1, 8):
-        sm_z(n, z).start()
-
-    ag_core(1, 1 - c).wait_recv()
-    ag_core(0, 1 - c).wait_recv()
-    for m in range(2):
-        reduce_out(m).start()
-
-    for n in range(1, 8):
-        sm_z(n, (z + 8 - n) % 8).wait_recv()
-    whole = smz[0]
-    for n in range(1, 8):
-        whole = whole + smz[n]
-    row = lax.broadcasted_iota(jnp.int32, (8, 640), 0)
-    smf[c] = jnp.where(row == 7, smz[z], whole)
-    sm_last(c).start()
 
     @pl.loop(0, HOPS)
     def _(hop):
@@ -492,13 +508,19 @@
         sm_x(n, me_x, x_devices[n]).wait_send()
     for n in range(1, 8):
         sm_z(n, z).wait_send()
+    for n in range(1, 8):
+        sm_z(n, (z + 8 - n) % 8).wait_recv()
+    whole = added_up(smz, 8)
+    row = lax.broadcasted_iota(jnp.int32, (16, 640), 0)
+    whole = jnp.where(row % 8 == 7, smz[z].astype(F32), whole)
+    sm_ref[:, 0:640] = whole[0:8]
+    sm_ref[:, 640:1280] = whole[8:16]
+    last = sm_ref[7:8, :]
+    sm_ref[7:8, 0:H] = jnp.where(xh == 0, last[:, 0:H], last[:, 384:384 + H])
     gi_out.wait()
     for m in range(2):
-        reduce_out(m).wait()
-    sm_last(1 - c).wait_recv()
-    sm_ref[...] = smf[...]
-    sm_last(c).wait_send()
-
+        for half in range(2):
+            reduce_out(m, half).wait()
 
 def shards(inputs, saved_hidden, upstream, w_in, w_out, kernel):
     anyspace = pl.BlockSpec(memory_space=pl.ANY)
@@ -508,9 +530,9 @@
         body,
         out_shape=(
             jax.ShapeDtypeStruct((1, T, D), BF16),
-            jax.ShapeDtypeStruct((2, 4, 80, 640), BF16),
-            jax.ShapeDtypeStruct((2, 4, 80, 640), BF16),
-            jax.ShapeDtypeStruct((2, 8, 640), F32),
+            jax.ShapeDtypeStruct((H, D), BF16),
+            jax.ShapeDtypeStruct((H, D), BF16),
+            jax.ShapeDtypeStruct((8, D), F32),
         ),
         in_specs=[anyspace] * 5 + [vmem],
         out_specs=(anyspace, anyspace, anyspace, vmem),
@@ -519,11 +541,13 @@
             pltpu.VMEM((SLOTS, SR, D), BF16),
             pltpu.VMEM((SLOTS, SR, D), BF16),
             pltpu.VMEM((HOPS, SR, D), BF16),
-            pltpu.VMEM((2, SLOTS, SR, H), BF16),
+            pltpu.VMEM((8, H, 2 * T), BF16),
+            pltpu.VMEM((8, 2 * T, H), BF16),
+            pltpu.VMEM((SLOTS, SR, H), BF16),
             pltpu.VMEM((2, SLOTS, SR, H), BF16),
             pltpu.VMEM((2, SLOTS, SR, H), BF16),
             pltpu.VMEM((2, H, D), BF16),
-            pltpu.VMEM((2, D, H), BF16),
+            pltpu.VMEM((2, H, D), BF16),
             pltpu.VMEM((2, H, D), F32),
             pltpu.VMEM((2, H, D), F32),
             pltpu.VMEM((H, 8 * SR), BF16),
@@ -534,7 +558,7 @@
             pltpu.VMEM((2, 3, 2, 80, 640), BF16),
             pltpu.VMEM((2, 2, 80, 640), BF16),
             pltpu.VMEM((2, 4, 80, 640), BF16),
-            pltpu.VMEM((2, 2, 4, 80, 640), BF16),
+            pltpu.VMEM((2, 2, H, 640), BF16),
             pltpu.VMEM((T + 2 * HALO, D), BF16),
             pltpu.VMEM((T + 2 * HALO, D), F32),
             pltpu.VMEM((T + 2 * HALO, D), F32),
@@ -542,28 +566,23 @@
             pltpu.VMEM((T, D), BF16),
             pltpu.VMEM((2, HALO, D), BF16),
             pltpu.VMEM((8, D), F32),
-            pltpu.VMEM((8, D), F32),
-            pltpu.VMEM((4, 8, 640), F32),
-            pltpu.VMEM((4, 8, 640), F32),
-            pltpu.VMEM((8, 8, 640), F32),
-            pltpu.VMEM((2, 8, 640), F32),
+            pltpu.VMEM((16, 640), BF16),
+            pltpu.VMEM((16, 640), BF16),
+            pltpu.VMEM((4, 16, 640), BF16),
+            pltpu.VMEM((4, 16, 640), BF16),
+            pltpu.VMEM((8, 16, 640), BF16),
             dma((3, HOPS, 2)), dma((3, HOPS, 2)),
-            dma((SLOTS, 2)), dma((SLOTS, 2)), dma((SLOTS, 2)),
-            dma((2,)), dma((2,)), dma((7,)), dma((3,)),
+            dma((SLOTS, 2)), dma((SLOTS, 2)), dma((8,)),
+            dma((2,)), dma((2,)), dma((7,)), dma((3, 2)),
             dma((4,)), dma((4,)),
             dma((2, 11)), dma((2, 11)),
-            dma((15,)), dma((15,)),
+            dma((14,)), dma((14,)),
         ],
         compiler_params=pltpu.CompilerParams(
             collective_id=0, has_side_effects=True, vmem_limit_bytes=64 * 1024 * 1024 - 65536),
         name="step",
-    )(inputs, saved_hidden, upstream, w_in, w_out, kernel)
-    grad_w_out = jnp.concatenate([gwo[0].reshape(H, 640), gwo[1].reshape(H, 640)], axis=1).astype(F32)
-    grad_w_in = gwi.reshape(2, H, 640).transpose(0, 2, 1).reshape(D, H).astype(F32)
-    small = jnp.concatenate([small[0], small[1]], axis=1)
-    parity = lax.axis_index("tp") % 2
-    grad_bias = jnp.where(parity == 0, small[7, :H], small[7, 384:384 + H])
-    return grad_inputs, grad_w_in, grad_w_out, grad_bias, small[:KW]
+    )(inputs, jnp.swapaxes(saved_hidden, 1, 2), upstream, w_in.T, w_out, kernel)
+    return grad_inputs, gwi.astype(F32).T, gwo.astype(F32), small[7, :H], small[:KW]
 
 
 def solution(mesh):

time: 166 us -> 153 us (0.922); the launches traced: 164 us -> 153 us
  local copies, waits for them, and re-layouts: 7.71 us -> 2 us
  Pallas kernels: 152 us -> 147 us
    unnamed x11 -> x8, local copies, waits for them, and re-layouts: 6.35 us -> 1.41 us
    pallas_call x1, Pallas kernels: 152 us -> 147 us  [shards(): pl.pallas_call(body, out_shape=(jax.ShapeDtypeStruct((1, T, D), BF16), ja...]
    transpose x0 -> x1, other arithmetic: none -> 2.49 us  [shards(): gwi.astype(F32)]
where the time goes in v2:
time: 153 us
  Pallas kernels  147 us (96%)
  other arithmetic  3.76 us (2%)
  local copies, waits for them, and re-layouts  2 us (1%)
    pallas_call x1, Pallas kernels, shards(): pl.pallas_call(body, out_shape=(jax.ShapeDtypeStruct((1, T, D), BF16), ja...  147 us

profile of v2, /device:TPU:2, one launch (start us, length us, event | category | flops | bytes accessed | tf_op | source)
XLA Modules:
  0.0 153.2 jit_solution(5269699787824194744)
XLA Ops:
  0.6 146.8 %step.1 = (bf16[1,192,1280]{2,1,0:T(8,128)(2,1)}, bf16[320,1280]{1,0:T(8,128)(2,1)}, bf16[320,1280]{1,0:T(8,128)(2,1)}, f32[8,1280]{1,0:T(8,128)}) custom-call(bf16[1,192,1280]{2,1,0:T(8,128)(2,1)} %x_hbm.1, bf16[1,320,3072]{2,1,0:T(8,128)(2,1)} %bitcast.5, bf16[1,192,1280]{2,1,0:T(8,128)(2,1)} %u_hbm.1, bf16[320,1280]{1,0:T(8,128)(2,1)} %bitcast.6, ...), custom_call_target="tpu_custom_call" | custom-call | tf_op jit(solution)/shard_map/step/pallas_call | solution.py:529
  147.4 0.0 copy-start
  147.4 2.5 %convert_bitcast_fusion = f32[1280,320]{0,1:T(8,128)} fusion(bf16[320,1280]{1,0:T(8,128)(2,1)} %get-tuple-element.10), kind=kLoop, calls=%fused_computation | loop fusion | flops 409600 | bytes 2457600 | tf_op jit(solution)/shard_map/transpose | solution.py:585
  149.9 0.0 copy-start.2
  149.9 0.0 copy-start.1
  149.9 0.0 copy-done
  149.9 1.3 convert_element_type.4
  151.2 0.0 copy-done.2
  151.2 0.6 slice_reduce_fusion
  151.8 0.0 copy-done.1
  151.8 0.8 copy.13
  152.6 0.6 copy.14
Async XLA Ops:
  147.4 2.5 %copy-start = (bf16[320,1280]{1,0:T(8,128)(2,1)S(1)}, bf16[320,1280]{1,0:T(8,128)(2,1)}, u32[]{:S(2)}) copy-start(bf16[320,1280]{1,0:T(8,128)(2,1)} %get-tuple-element.11) | copy-start | bytes 2457604
  149.9 1.3 copy-start.2
  149.9 1.9 %copy-start.1 = (bf16[1,192,1280]{2,1,0:T(8,128)(2,1)S(1)}, bf16[1,192,1280]{2,1,0:T(8,128)(2,1)}, u32[]{:S(2)}) copy-start(bf16[1,192,1280]{2,1,0:T(8,128)(2,1)} %get-tuple-element.18) | copy-start | bytes 1474564

commit v3 on v2

v3 whole, which is shorter than its diff:
```python
import functools

import jax
import jax.numpy as jnp
from jax import lax
from jax.experimental import pallas as pl
from jax.experimental.pallas import tpu as pltpu
from jax.sharding import PartitionSpec as P

KW = 7
D = 1280
H = 320
T = 192
SLOTS = 16
HR = 48
HC = D // 2
SR = 2 * HR
HOPS = SLOTS - 2
HALO = 16
MESH_ID = pl.DeviceIdType.MESH
F32 = jnp.float32
BF16 = jnp.bfloat16

LAG = 6
RELAY_AT = (4, 18)
GWO_AT = ((14, 15), (22, 23))
DX_FROM = 20
GWI_AT = (((0, 0), 25), ((1, 1), 28), ((0, 1), 30), ((1, 0), 31))
TAPS_FROM = 28
SMALL_AT = (36, 37, 39, 41)
RED_AT = ((24, 26, 32, 35, 39), (31, 32, 37, 40, None))
STEPS = 3 * HOPS + 2


def dot_nt(a, b):
    return lax.dot_general(a, b, (((1,), (1,)), ((), ())), preferred_element_type=F32)


def gelu_parts(x):
    a = jnp.abs(x) * 0.7071067811865476
    t = 1.0 / (1.0 + 0.5 * a)
    p = 0.17087277
    for coef in (
        -0.82215223,
        1.48851587,
        -1.13520398,
        0.27886807,
        -0.18628806,
        0.09678418,
        0.37409196,
        1.00002368,
        -1.26551223,
    ):
        p = p * t + coef
    square = a * a
    tail = 0.5 * t * jnp.exp(p - square)
    cdf = jnp.where(x >= 0, 1.0 - tail, tail)
    slope = cdf + x * (0.3989422804014327 * jnp.exp(-square))
    return x * cdf, slope


def body(
    x_hbm, h_hbm, u_hbm, wi_hbm, wo_hbm, k_ref,
    gm_hbm, gwo_hbm, gwi_hbm, sm_ref,
    up, xg, mx, dx, rr, ht, hrow, hh, act, gh, wo, wi, gwo, gwi, actt, bias,
    cs, cr, ys, yr, xs, xr, fout,
    xf, gx, gmb, gib, sm, sms, smc, smy, smx, smp, smz, smg,
    z_send, z_recv, h_send, h_recv, h_load, w_send, w_recv, l_sem, o_sem,
    halo_send, halo_recv, edge_send, edge_recv, red_send, red_recv, s_send, s_recv, zs_send, zs_recv, zg_send, zg_recv,
):
    dp, tp = lax.axis_index("dp"), lax.axis_index("tp")
    xl, y, c = dp // 8, (dp // 2) % 4, dp % 2
    z, xh = tp // 2, tp % 2
    me_x = xh * 2 + xl

    def z_dev(n):
        return (dp, (tp + 2 * n + 32) % 16)

    def y_dev(n):
        return (xl * 8 + ((y + n) % 4) * 2 + c, tp)

    core_dev = (dp + 1 - 2 * c, tp)
    xh_dev = (dp, tp + 1 - 2 * xh)
    xl_dev = (dp + 8 - 16 * xl, tp)
    xd_dev = (dp + 8 - 16 * xl, tp + 1 - 2 * xh)
    next_dev = (dp, (tp + 1) % 16)
    prev_dev = (dp, (tp + 15) % 16)

    def remote(src, dst, send, recv, device):
        return pltpu.make_async_remote_copy(
            src_ref=src, dst_ref=dst, send_sem=send, recv_sem=recv,
            device_id=device, device_id_type=MESH_ID,
        )

    def local_loads():
        copies = []
        n = 0
        for a in range(2):
            for half in range(2):
                copies.append(pltpu.make_async_copy(
                    u_hbm.at[0, pl.ds(half * 96 + a * HR, HR)], up.at[a, pl.ds(half * HR, HR)], l_sem.at[n]))
                n += 1
        for half in range(2):
            copies.append(pltpu.make_async_copy(
                x_hbm.at[0, :, pl.ds(half * HC, HC)], xg.at[half, 0, pl.ds(HALO, T)], l_sem.at[n]))
            n += 1
        copies.append(pltpu.make_async_copy(wo_hbm, wo.at[0], l_sem.at[n]))
        copies.append(pltpu.make_async_copy(wi_hbm, wi.at[0], l_sem.at[n + 1]))
        return copies

    def hidden_chunk(n):
        return (z + 8 + ((n + 1) // 2) * (1 - 2 * (n % 2))) % 8

    def hidden_load(n):
        chunk = hidden_chunk(n)
        cols = pl.ds(pl.multiple_of(chunk * 2 * T, 128), 2 * T)
        return pltpu.make_async_copy(h_hbm.at[0, :, cols], ht.at[chunk], h_load.at[n])

    def hidden_rows(slot, half, parity):
        s, a = slot // 2, slot % 2
        chunk = (z + (s if half else 8 - s)) % 8
        return chunk, pl.ds(pl.multiple_of(parity * T + half * 96 + a * HR, 16), HR)

    def hidden_send(slot, half):
        chunk, rows = hidden_rows(slot, half, 1 - xh)
        return remote(
            hrow.at[chunk, rows], hh.at[slot, pl.ds(half * HR, HR)],
            h_send.at[slot, half], h_recv.at[slot, half], xh_dev)

    own_half = pl.ds(c * 160, 160)
    other_half = pl.ds((1 - c) * 160, 160)

    def weight_copy(n):
        source, held = ((wo_hbm, wo), (wi_hbm, wi))[n]
        return remote(source.at[own_half], held.at[1, own_half], w_send.at[n, 0], w_recv.at[n, 0], xh_dev)

    def weight_relay(n, half):
        held = (wo, wi)[n]
        return remote(held.at[1, half], held.at[1, half], w_send.at[n, 1], w_recv.at[n, 1], core_dev)

    def edge_to(slot, half, a):
        step = 1 if half == a else 7
        return (slot + (xh if a else 1 - xh) * step) % 8

    def edge_send_copy(slot, half, a):
        rows = pl.ds(HALO + (T - HALO if a else 0), HALO)
        target = edge_to(slot, half, a)
        return remote(
            xg.at[half, slot, rows], xg.at[half, target, pl.ds(0 if a else T + HALO, HALO)],
            edge_send.at[half, a, slot], edge_recv.at[half, a, target], xh_dev)

    def edge_do(slot, half, a, act_on):
        @pl.when(edge_to(slot, half, a) != 0)
        def _():
            act_on(edge_send_copy(slot, half, a))

    def first_edge(half, a):
        cols = pl.ds(half * HC, HC)
        return remote(
            x_hbm.at[0, pl.ds(T - HALO if a else 0, HALO), cols],
            xg.at[half, 0, pl.ds(0 if a else T + HALO, HALO)],
            halo_send.at[half, a], edge_recv.at[half, a, 0], next_dev if a else prev_dev)

    def edge_arrival(slot, half, a):
        return remote(
            xg.at[half, slot, pl.ds(HALO, HALO)], xg.at[half, slot, pl.ds(0 if a else T + HALO, HALO)],
            edge_send.at[half, a, slot], edge_recv.at[half, a, slot], xh_dev)

    def ring(phase, hop, half, first=True):
        device = z_dev(-1 if half else 1)
        s, a = hop // 2, hop % 2
        if phase == 0:
            rows = pl.ds(half * HR, HR)
            src, dst = up.at[hop, rows], up.at[hop + 2, rows]
        elif phase == 1:
            rows = pl.ds(pl.multiple_of(HALO + a * SR, 16), SR)
            src, dst = xg.at[half, s, rows], xg.at[half, s + 1, rows]
        else:
            rows = pl.ds(pl.multiple_of(a * SR, 16), SR)
            src = dx.at[half, 7 if half else 1, rows] if first else rr.at[half, s - 1, rows]
            dst = rr.at[half, s, rows]
        return remote(src, dst, z_send.at[phase, hop, half], z_recv.at[phase, hop, half], device)

    locals_ = local_loads()
    for copy in locals_:
        copy.start()
    for n in range(8):
        hidden_load(n).start()
    barrier = pltpu.get_barrier_semaphore()
    peers = [z_dev(1), z_dev(-1)] + [y_dev(n) for n in range(1, 4)]
    peers += [core_dev, xl_dev, xh_dev, xd_dev, next_dev, prev_dev]
    for peer in peers:
        pl.semaphore_signal(barrier, inc=1, device_id=peer, device_id_type=MESH_ID)
    pl.semaphore_wait(barrier, len(peers))

    weight_copy(0).start()
    for half in range(2):
        locals_[4 + half].wait()
        for a in range(2):
            first_edge(half, a).start()
            edge_do(0, half, a, lambda copy: copy.start())

    sm[...] = jnp.zeros_like(sm)
    bias[...] = jnp.zeros_like(bias)

    def red_core(m):
        return remote(cs.at[m, 1 - c], cr.at[m], red_send.at[m, 0], red_recv.at[m, 0], core_dev)

    def red_y(m, n):
        return remote(ys.at[m, (y + n) % 4], yr.at[m, n - 1], red_send.at[m, n], red_recv.at[m, n], y_dev(n))

    def red_x(m):
        return (
            remote(xs.at[m, 0], xr.at[m, me_x], red_send.at[m, 4], red_recv.at[m, 4], xl_dev),
            remote(xs.at[m, 1], xr.at[m, me_x], red_send.at[m, 5], red_recv.at[m, 5], xh_dev),
            remote(xs.at[m, 1], xr.at[m, me_x], red_send.at[m, 6], red_recv.at[m, 6], xd_dev),
        )

    def red_x_wait(m):
        for sem, src_x, device in (
            (4, xh * 2 + 1 - xl, xl_dev), (5, (1 - xh) * 2 + xl, xh_dev), (6, (1 - xh) * 2 + 1 - xl, xd_dev),
        ):
            remote(xs.at[m, 0], xr.at[m, src_x], red_send.at[m, sem], red_recv.at[m, sem], device).wait_recv()

    def ag_y(m, n, source):
        return remote(
            fout.at[m, c, pl.ds(source * 80, 80)], fout.at[m, c, pl.ds(source * 80, 80)], red_send.at[m, 6 + n], red_recv.at[m, 6 + n], y_dev(n))

    def ag_core(m, half):
        return remote(fout.at[m, half], fout.at[m, half], red_send.at[m, 10], red_recv.at[m, 10], core_dev)

    totals = (gwo, gwi)

    def reduce_stage(m, stage):
        total = totals[m]
        if stage == 0:
            for q in range(2):
                for half in range(2):
                    cs[m, half, q] = total[q, :, half * 640:(half + 1) * 640].astype(BF16)
            red_core(m).start()
        elif stage == 1:
            red_core(m).wait_recv()
            own_cols = pl.ds(pl.multiple_of(c * 640, 128), 640)
            for q in range(2):
                for part in range(4):
                    rows = slice(part * 80, part * 80 + 80)
                    ys[m, part, q] = (total[q, rows, own_cols] + cr[m, q, rows].astype(F32)).astype(BF16)
            for n in range(1, 4):
                red_y(m, n).start()
        elif stage == 2:
            for n in range(1, 4):
                red_y(m, n).wait_recv()
            for q in range(2):
                part = ys[m, y, q].astype(F32)
                for n in range(3):
                    part = part + yr[m, n, q].astype(F32)
                xs[m, q] = part.astype(BF16)
            for copy in red_x(m):
                copy.start()
        elif stage == 3:
            red_x_wait(m)
            xr[m, me_x] = xs[m, 0]
            part = xr[m, 0].astype(F32)
            for n in range(1, 4):
                part = part + xr[m, n].astype(F32)
            fout[m, c, pl.ds(y * 80, 80)] = part.astype(BF16)
            for n in range(1, 4):
                ag_y(m, n, y).start()
        else:
            for n in range(1, 4):
                ag_y(m, n, (y + 4 - n) % 4).wait_recv()
            ag_core(m, c).start()

    def reduce_out(m, half):
        cols = pl.ds(half * 640, 640)
        return pltpu.make_async_copy(fout.at[m, half], (gwo_hbm, gwi_hbm)[m].at[:, cols], o_sem.at[m, half])

    def widen(slot, half):
        block = 2 * ((z + (slot if half else 8 - slot)) % 8) + xh
        xf[pl.ds(HALO, T)] = xg[half, slot, pl.ds(HALO, T)].astype(F32)
        xf[pl.ds(0, HALO)] = jnp.where(block == 0, 0.0, xg[half, slot, pl.ds(0, HALO)].astype(F32))
        xf[pl.ds(T + HALO, HALO)] = jnp.where(block == 15, 0.0, xg[half, slot, pl.ds(T + HALO, HALO)].astype(F32))

    def mixed_task(slot, half):
        for a in range(2):
            edge_arrival(slot, half, a).wait_recv()
        widen(slot, half)
        place = (8 - slot) % 8 if half else slot

        @pl.loop(0, HC // 128)
        def _(n):
            cols = pl.ds(pl.multiple_of(n * 128, 128), 128)
            taps = k_ref[:, pl.ds(pl.multiple_of(half * HC + n * 128, 128), 128)]
            out = xf[HALO:HALO + T, cols]
            for tap in range(KW):
                out = out + taps[tap:tap + 1] * xf[HALO - 3 + tap:HALO - 3 + tap + T, cols]
            mx[half, place, :, cols] = out.astype(BF16)

    def taps_task(place, own):
        for half in range(2):
            widen((8 - place) % 8 if half else place, half)
            gx[...] = dx[half, place].astype(F32)

            @pl.when(own)
            def _():
                for a in range(2):
                    for part in range(2):
                        start = part * 96 + a * HR
                        gx[start:start + HR] += up[a, part * HR:(part + 1) * HR, half * HC:(half + 1) * HC].astype(F32)

            @pl.loop(0, HC // 128)
            def _(n):
                cols = pl.ds(pl.multiple_of(n * 128, 128), 128)
                into = pl.ds(pl.multiple_of(half * HC + n * 128, 128), 128)
                grad = gx[:, cols]
                for tap in range(KW):
                    product = grad * xf[HALO - 3 + tap:HALO - 3 + tap + T, cols]
                    sm[tap:tap + 1, into] += jnp.sum(product, axis=0, keepdims=True)

    def place_order(n):
        return (n % 2) * (4 + n // 2) + (1 - n % 2) * ((4 - n // 2) % 4)

    def hidden_task(slot):
        for half in range(2):
            hidden_send(slot, half).wait_recv()
        gathered = up[slot]
        own = []
        for half in range(2):
            chunk, where = hidden_rows(slot, half, xh)
            own.append(hrow[chunk, where])
        own = jnp.concatenate(own, axis=0)
        for q in range(2):
            back = dot_nt(gathered, wo[q])
            value, slope = gelu_parts((hh[slot] if q else own).astype(F32))
            grad = (slope * back).astype(BF16)
            act[q, slot] = value.astype(BF16)
            for half in range(2):
                place = (8 - slot // 2) % 8 if half else slot // 2
                rows = pl.ds(pl.multiple_of(half * 96 + (slot % 2) * HR, 16), HR)
                gh[q, place, rows] = grad[half * HR:(half + 1) * HR]
            bias[q] += jnp.sum(grad.astype(F32).reshape(SR // 8, 8, H), axis=0)

    def out_weight_task(q, part):
        eight = pl.ds(part * 8, 8)
        actt[...] = act[q, eight].reshape(8 * SR, H).T

        @pl.loop(0, D // 256)
        def _(n):
            cols = pl.ds(pl.multiple_of(n * 256, 256), 256)
            value = jnp.dot(
                actt[...], up[eight, :, cols].reshape(8 * SR, 256), preferred_element_type=F32)
            if part == 0:
                gwo[q, :, cols] = value
            else:
                gwo[q, :, cols] += value

    def in_weight_task(half, part):
        four = pl.ds(part * 4, 4)
        for q in range(2):
            actt[...] = gh[q, four].reshape(4 * T, H).T
            for start, width in ((0, 256), (256, 256), (512, 128)):
                value = jnp.dot(
                    actt[...], mx[half, four, :, start:start + width].reshape(4 * T, width),
                    preferred_element_type=F32)
                cols = slice(half * HC + start, half * HC + start + width)
                if part == half:
                    gwi[q, :, cols] = value
                else:
                    gwi[q, :, cols] += value

    def dx_task(place):
        g0, g1 = gh[0, place], gh[1, place]
        for start, width in ((0, 256), (256, 256), (512, 128), (640, 256), (896, 256), (1152, 128)):
            cols = slice(start, start + width)
            half = start // HC
            dx[half, place, :, start - half * HC:start - half * HC + width] = (
                jnp.dot(g0, wi[0, :, cols], preferred_element_type=F32)
                + jnp.dot(g1, wi[1, :, cols], preferred_element_type=F32)
            ).astype(BF16)

    def sm_core():
        return remote(sms, smc, s_send.at[0], s_recv.at[0], core_dev)

    def sm_y(n, source):
        return remote(smy.at[source], smy.at[source], s_send.at[n], s_recv.at[n], y_dev(n))

    def sm_x(n, source, device):
        return remote(smx.at[source], smx.at[source], s_send.at[4 + n], s_recv.at[4 + n], device)

    def sm_scatter(piece, source):
        return remote(smp.at[piece], smz.at[source], zs_send.at[piece], zs_recv.at[source], (dp, 2 * piece + xh))

    def sm_gather(n, piece):
        return remote(smg.at[piece], smg.at[piece], zg_send.at[n], zg_recv.at[piece], z_dev(n))

    x_devices = (xl_dev, xh_dev, xd_dev)

    def added_up(ref, count):
        total = ref[0].astype(F32)
        for n in range(1, count):
            total = total + ref[n].astype(F32)
        return total

    def small_stage(stage):
        if stage == 0:
            b0 = jnp.sum(bias[0], axis=0, keepdims=True)
            b1 = jnp.sum(bias[1], axis=0, keepdims=True)
            sm[7:8, 0:H] = jnp.where(xh == 0, b0, b1)
            sm[7:8, 384:384 + H] = jnp.where(xh == 0, b1, b0)
            sms[0:8] = sm[:, 0:640].astype(BF16)
            sms[8:16] = sm[:, 640:1280].astype(BF16)
            sm_core().start()
        elif stage == 1:
            sm_core().wait_recv()
            smy[y] = (sms[...].astype(F32) + smc[...].astype(F32)).astype(BF16)
            for n in range(1, 4):
                sm_y(n, y).start()
        elif stage == 2:
            for n in range(1, 4):
                sm_y(n, (y + 4 - n) % 4).wait_recv()
            smx[me_x] = added_up(smy, 4).astype(BF16)
            for n in range(3):
                sm_x(n, me_x, x_devices[n]).start()
        else:
            for n, source in enumerate((xh * 2 + 1 - xl, (1 - xh) * 2 + xl, (1 - xh) * 2 + 1 - xl)):
                sm_x(n, source, x_devices[n]).wait_recv()
            total = added_up(smx, 4).astype(BF16)
            for piece in range(5):
                smp[piece] = total[:, piece * 128:piece * 128 + 128]
            for piece in range(5):
                @pl.when(z != piece)
                def _():
                    sm_scatter(piece, z).start()

    def small_gather():
        @pl.when(z < 5)
        def _():
            for n in range(1, 8):
                source = (z + n) % 8
                remote(smp.at[0], smz.at[source], zs_send.at[0], zs_recv.at[source], z_dev(n)).wait_recv()
            smz[z] = smp[z]
            smg[z] = added_up(smz, 8).astype(BF16)
            for n in range(1, 8):
                sm_gather(n, z).start()

    for n in range(4):
        locals_[n].wait()

    def at(step, i):
        return pl.when(i == step)

    def step(i, carry):
        for half in range(2):
            @pl.when((i >= 2) & (i < 16))
            def _():
                ring(0, i - 2, half).wait_recv()

            @pl.when(i < HOPS)
            def _():
                ring(0, i, half).start()

        for half in range(2):
            @pl.when((i >= 16) & (i < 30))
            def _():
                ring(1, i - 16, half).wait_recv()

            @pl.when((i >= 14) & (i < 28))
            def _():
                ring(1, i - 14, half).start()

        @pl.when((i >= 30) & (i < 42))
        def _():
            s = (i - 28) // 2
            rows = pl.ds(pl.multiple_of((i % 2) * SR, 16), SR)
            for half in range(2):
                ring(2, i - 30, half).wait_recv()
                place = 7 - s if half else s + 1
                rr[half, s - 1, rows] = (
                    rr[half, s - 1, rows].astype(F32) + dx[half, place, rows].astype(F32)).astype(BF16)
                ring(2, i - 28, half, first=False).start()

        @pl.when((i >= 28) & (i < 30))
        def _():
            for half in range(2):
                ring(2, i - 28, half).start()

        @pl.when((i >= 16) & (i < 30))
        def _():
            slot = (i - 16) // 2 + 1
            for a in range(2):
                @pl.when(i % 2 == a)
                def _():
                    for half in range(2):
                        edge_do(slot, half, a, lambda copy: copy.start())

        @pl.when(i < 8)
        def _():
            hidden_load(i).wait()
            chunk = hidden_chunk(i)
            hrow[chunk] = ht[chunk].T

        @pl.when((i < 8) & (i % 2 == 0))
        def _():
            for j in range(2):
                for half in range(2):
                    hidden_send(i + j, half).start()

        @at(7, i)
        def _():
            @pl.loop(8, SLOTS)
            def _(slot):
                for half in range(2):
                    hidden_send(slot, half).start()

        for n in range(2):
            @at(RELAY_AT[n], i)
            def _():
                weight_copy(n).wait_recv()
                weight_relay(n, own_half).start()

        @at(8, i)
        def _():
            weight_copy(1).start()

        @at(LAG, i)
        def _():
            locals_[6].wait()
            weight_relay(0, other_half).wait_recv()

        for half in range(2):
            @pl.when((i >= 18) & (i < 32) & (i % 2 == half))
            def _():
                mixed_task((i - 18) // 2, half)

            at(30 + half, i)(functools.partial(mixed_task, 7, half))

        @pl.when((i >= LAG) & (i < LAG + SLOTS))
        def _():
            hidden_task(i - LAG)

        for part in range(2):
            for q in range(2):
                at(GWO_AT[part][q], i)(functools.partial(out_weight_task, q, part))
        for which, when in GWI_AT:
            at(when, i)(functools.partial(in_weight_task, *which))

        @at(DX_FROM, i)
        def _():
            locals_[7].wait()
            weight_relay(1, other_half).wait_recv()

        @pl.when((i >= DX_FROM) & (i < DX_FROM + 8))
        def _():
            dx_task(place_order(i - DX_FROM))

        @pl.when((i >= TAPS_FROM) & (i < TAPS_FROM + 8))
        def _():
            taps_task(place_order(i - TAPS_FROM), i == TAPS_FROM)

        for stage in range(4):
            at(SMALL_AT[stage], i)(functools.partial(small_stage, stage))

        for m in range(2):
            for stage in range(5):
                if RED_AT[m][stage] is not None:
                    at(RED_AT[m][stage], i)(functools.partial(reduce_stage, m, stage))
        return carry

    lax.fori_loop(0, STEPS - 2, step, 0)

    edge_copies = (
        remote(gmb.at[pl.ds(T - HALO, HALO)], gib.at[0], halo_send.at[2, 0], halo_recv.at[0], next_dev),
        remote(gmb.at[pl.ds(0, HALO)], gib.at[1], halo_send.at[2, 1], halo_recv.at[1], prev_dev),
    )
    for a in range(2):
        rows = slice(a * SR, a * SR + SR)
        for half in range(2):
            ring(2, HOPS - 2 + a, half).wait_recv()
            cols = slice(half * HC, half * HC + HC)
            own = jnp.concatenate([up[n, a * HR:a * HR + HR, cols] for n in range(2)], axis=0).astype(F32)
            done = own + (dx[half, 0, rows].astype(F32) + rr[half, 6, rows].astype(F32))
            done = done.astype(BF16)
            gmb[rows, cols] = done
        edge_copies[1 - a].start()
    gm_out = [pltpu.make_async_copy(gmb, gm_hbm.at[pl.ds(HALO, T)], o_sem.at[2, 0])]
    gm_out[0].start()
    ag_core(0, 1 - c).wait_recv()
    for half in range(2):
        reduce_out(0, half).start()
    small_gather()
    reduce_stage(1, 4)
    for copy in edge_copies:
        copy.wait_recv()
    gib[0] = jnp.where(tp == 0, 0.0, gib[0].astype(F32)).astype(BF16)
    gib[1] = jnp.where(tp == 15, 0.0, gib[1].astype(F32)).astype(BF16)
    for n, row in enumerate((0, T + HALO)):
        gm_out.append(pltpu.make_async_copy(gib.at[n], gm_hbm.at[pl.ds(row, HALO)], o_sem.at[3, n]))
        gm_out[-1].start()
    ag_core(1, 1 - c).wait_recv()
    for half in range(2):
        reduce_out(1, half).start()

    @pl.loop(0, HOPS)
    def _(hop):
        for phase in range(3):
            for half in range(2):
                ring(phase, hop, half).wait_send()

    @pl.loop(0, SLOTS)
    def _(slot):
        for half in range(2):
            hidden_send(slot, half).wait_send()

    for n in range(2):
        weight_copy(n).wait_send()
        weight_relay(n, own_half).wait_send()
    for copy in edge_copies:
        copy.wait_send()
    for half in range(2):
        for a in range(2):
            first_edge(half, a).wait_send()

    @pl.loop(0, 8)
    def _(slot):
        for half in range(2):
            for a in range(2):
                edge_do(slot, half, a, lambda copy: copy.wait_send())

    for m in range(2):
        red_core(m).wait_send()
        for n in range(1, 4):
            red_y(m, n).wait_send()
            ag_y(m, n, y).wait_send()
        for copy in red_x(m):
            copy.wait_send()
        ag_core(m, c).wait_send()
    sm_core().wait_send()
    for n in range(1, 4):
        sm_y(n, y).wait_send()
    for n in range(3):
        sm_x(n, me_x, x_devices[n]).wait_send()
    row = lax.broadcasted_iota(jnp.int32, (16, 128), 0)
    for piece in range(5):
        @pl.when(z != piece)
        def _():
            sm_scatter(piece, z).wait_send()
            sm_gather(1, piece).wait_recv()

        whole = jnp.where(row % 8 == 7, smp[piece].astype(F32), smg[piece].astype(F32))
        sm_ref[:, piece * 128:piece * 128 + 128] = whole[0:8]
        sm_ref[:, piece * 128 + 640:piece * 128 + 768] = whole[8:16]

    @pl.when(z < 5)
    def _():
        for n in range(1, 8):
            sm_gather(n, z).wait_send()

    last = sm_ref[7:8, :]
    sm_ref[7:8, 0:H] = jnp.where(xh == 0, last[:, 0:H], last[:, 384:384 + H])
    for copy in gm_out:
        copy.wait()
    for m in range(2):
        for half in range(2):
            reduce_out(m, half).wait()

def finish(gm_hbm, gwo_hbm, gwi_hbm, sm_ref, k_ref, gi_out, gwo_out, gwi_out, taps_ref, bias_ref,
           gb, gf, gio, narrow, wide, in_sem, out_sem):
    loads, stores = [], []
    for n in range(4):
        rows = pl.ds((n % 2) * 160, 160)
        loads.append(pltpu.make_async_copy((gwo_hbm, gwi_hbm)[n // 2].at[rows], narrow.at[n], in_sem.at[n]))
        stores.append(pltpu.make_async_copy(wide.at[n], (gwo_out, gwi_out)[n // 2].at[rows], out_sem.at[n]))
        loads[n].start()
    loads.append(pltpu.make_async_copy(gm_hbm, gb, in_sem.at[4]))
    stores.append(pltpu.make_async_copy(gio, gi_out.at[0], out_sem.at[4]))
    loads[4].start()
    taps_ref[...] = sm_ref[0:KW]
    bias_ref[...] = sm_ref[KW, 0:H]
    for n in range(4):
        loads[n].wait()
        wide[n] = narrow[n].astype(F32)
        stores[n].start()
    loads[4].wait()
    gf[...] = gb[...].astype(F32)

    @pl.loop(0, D // 128)
    def _(n):
        cols = pl.ds(pl.multiple_of(n * 128, 128), 128)
        taps = k_ref[:, cols]
        out = gf[HALO:HALO + T, cols]
        for tap in range(KW):
            out = out + taps[tap:tap + 1] * gf[HALO + 3 - tap:HALO + 3 - tap + T, cols]
        gio[:, cols] = out.astype(BF16)

    stores[4].start()
    for store in stores:
        store.wait()


def shards(inputs, saved_hidden, upstream, w_in, w_out, kernel):
    anyspace = pl.BlockSpec(memory_space=pl.ANY)
    vmem = pl.BlockSpec(memory_space=pltpu.VMEM)
    dma = pltpu.SemaphoreType.DMA
    grad_mixed, gwo, gwi, small = pl.pallas_call(
        body,
        out_shape=(
            jax.ShapeDtypeStruct((T + 2 * HALO, D), BF16),
            jax.ShapeDtypeStruct((H, D), BF16),
            jax.ShapeDtypeStruct((H, D), BF16),
            jax.ShapeDtypeStruct((8, D), F32),
        ),
        in_specs=[anyspace] * 5 + [vmem],
        out_specs=(anyspace, anyspace, anyspace, vmem),
        scratch_shapes=[
            pltpu.VMEM((SLOTS, SR, D), BF16),
            pltpu.VMEM((2, 8, T + 2 * HALO, HC), BF16),
            pltpu.VMEM((2, 8, T, HC), BF16),
            pltpu.VMEM((2, 8, T, HC), BF16),
            pltpu.VMEM((2, 7, T, HC), BF16),
            pltpu.VMEM((8, H, 2 * T), BF16),
            pltpu.VMEM((8, 2 * T, H), BF16),
            pltpu.VMEM((SLOTS, SR, H), BF16),
            pltpu.VMEM((2, SLOTS, SR, H), BF16),
            pltpu.VMEM((2, 8, T, H), BF16),
            pltpu.VMEM((2, H, D), BF16),
            pltpu.VMEM((2, H, D), BF16),
            pltpu.VMEM((2, H, D), F32),
            pltpu.VMEM((2, H, D), F32),
            pltpu.VMEM((H, 8 * SR), BF16),
            pltpu.VMEM((2, 8, H), F32),
            pltpu.VMEM((2, 2, 2, H, 640), BF16),
            pltpu.VMEM((2, 2, H, 640), BF16),
            pltpu.VMEM((2, 4, 2, 80, 640), BF16),
            pltpu.VMEM((2, 3, 2, 80, 640), BF16),
            pltpu.VMEM((2, 2, 80, 640), BF16),
            pltpu.VMEM((2, 4, 80, 640), BF16),
            pltpu.VMEM((2, 2, H, 640), BF16),
            pltpu.VMEM((T + 2 * HALO, HC), F32),
            pltpu.VMEM((T, HC), F32),
            pltpu.VMEM((T, D), BF16),
            pltpu.VMEM((2, HALO, D), BF16),
            pltpu.VMEM((8, D), F32),
            pltpu.VMEM((16, 640), BF16),
            pltpu.VMEM((16, 640), BF16),
            pltpu.VMEM((4, 16, 640), BF16),
            pltpu.VMEM((4, 16, 640), BF16),
            pltpu.VMEM((5, 16, 128), BF16),
            pltpu.VMEM((8, 16, 128), BF16),
            pltpu.VMEM((5, 16, 128), BF16),
            dma((3, HOPS, 2)), dma((3, HOPS, 2)),
            dma((SLOTS, 2)), dma((SLOTS, 2)), dma((8,)),
            dma((2, 2)), dma((2, 2)), dma((8,)), dma((4, 2)),
            dma((3, 2)), dma((2,)), dma((2, 2, 8)), dma((2, 2, 8)),
            dma((2, 11)), dma((2, 11)),
            dma((7,)), dma((7,)), dma((5,)), dma((8,)), dma((8,)), dma((5,)),
        ],
        compiler_params=pltpu.CompilerParams(
            collective_id=0, has_side_effects=True, vmem_limit_bytes=64 * 1024 * 1024 - 65536),
        name="step",
    )(inputs, jnp.swapaxes(saved_hidden, 1, 2), upstream, w_in.T, w_out, kernel)
    grad_inputs, gwo, gwi, taps, bias = pl.pallas_call(
        finish,
        out_shape=(
            jax.ShapeDtypeStruct((1, T, D), BF16),
            jax.ShapeDtypeStruct((H, D), F32),
            jax.ShapeDtypeStruct((H, D), F32),
            jax.ShapeDtypeStruct((KW, D), F32),
            jax.ShapeDtypeStruct((H,), F32),
        ),
        in_specs=[anyspace] * 3 + [vmem, vmem],
        out_specs=(anyspace, anyspace, anyspace, vmem, vmem),
        scratch_shapes=[
            pltpu.VMEM((T + 2 * HALO, D), BF16),
            pltpu.VMEM((T + 2 * HALO, D), F32),
            pltpu.VMEM((T, D), BF16),
            pltpu.VMEM((4, 160, D), BF16),
            pltpu.VMEM((4, 160, D), F32),
            dma((5,)), dma((5,)),
        ],
        compiler_params=pltpu.CompilerParams(vmem_limit_bytes=64 * 1024 * 1024 - 65536),
        name="finish",
    )(grad_mixed, gwo, gwi, small, kernel)
    return grad_inputs, gwi.T, gwo, bias, taps


def solution(mesh):
    in_specs = (
        P("dp", "tp", None), P("dp", None, "tp"), P("dp", "tp", None), P(None, "tp"), P("tp", None), P())
    out_specs = (P("dp", "tp", None), P(None, "tp"), P("tp", None), P("tp"), P())
    return jax.shard_map(shards, mesh=mesh, in_specs=in_specs, out_specs=out_specs, check_vma=False)
```

time: 153 us -> 147 us (0.961)
  other arithmetic: 3.76 us -> 0 us
  Pallas kernels: 147 us -> 145 us
  local copies, waits for them, and re-layouts: 2 us -> 0 us
    transpose x1 -> x0, other arithmetic: 2.49 us -> none  [shards(): gwi.astype(F32)]
    pallas_call x1 -> x2, Pallas kernels: 147 us -> 145 us  [the longest x1 140 us: shards(): pl.pallas_call(body, out_shape=(jax.ShapeDtypeStruct((T + 2 * HALO, D), B...]
where the time goes in v3:
time: 147 us; the launch traced here: 146 us
  Pallas kernels  145 us (99%)
    pallas_call x1, Pallas kernels, shards(): pl.pallas_call(body, out_shape=(jax.ShapeDtypeStruct((T + 2 * HALO, D), B...  140 us
    pallas_call x1, Pallas kernels, shards(): pl.pallas_call(finish, out_shape=(jax.ShapeDtypeStruct((1, T, D), BF16),...  4.88 us

profile of v3, /device:TPU:2, one launch (start us, length us, event | category | flops | bytes accessed | tf_op | source)
XLA Modules:
  0.0 146.0 jit_solution(8303505660861189112)
XLA Ops:
  0.6 140.4 %step.1 = (bf16[224,1280]{1,0:T(8,128)(2,1)}, bf16[320,1280]{1,0:T(8,128)(2,1)}, bf16[320,1280]{1,0:T(8,128)(2,1)}, f32[8,1280]{1,0:T(8,128)}) custom-call(bf16[1,192,1280]{2,1,0:T(8,128)(2,1)} %x_hbm.1, bf16[1,320,3072]{2,1,0:T(8,128)(2,1)} %bitcast.3, bf16[1,192,1280]{2,1,0:T(8,128)(2,1)} %u_hbm.1, bf16[320,1280]{1,0:T(8,128)(2,1)} %bitcast.4, ...), custom_call_target="tpu_custom_call" | custom-call | tf_op jit(solution)/shard_map/step/pallas_call | solution.py:704
  141.1 4.9 %finish.1 = (bf16[1,192,1280]{2,1,0:T(8,128)(2,1)}, f32[320,1280]{1,0:T(8,128)}, f32[320,1280]{1,0:T(8,128)}, f32[7,1280]{1,0:T(8,128)}, f32[320]{0:T(512)}) custom-call(bf16[224,1280]{1,0:T(8,128)(2,1)} %get-tuple-element.14.gm_hbm, bf16[320,1280]{1,0:T(8,128)(2,1)} %get-tuple-element.15.gwo_hbm, bf16[320,1280]{1,0:T(8,128)(2,1)} %get-tuple-element.16.gwi_hbm, ...), custom_call_target="tpu_custom_call" | custom-call | tf_op jit(solution)/shard_map/finish/pallas_call | solution.py:761

commit v4 on v3

--- a/solution.py
+++ b/solution.py
@@ -28,7 +28,7 @@
 GWI_AT = (((0, 0), 25), ((1, 1), 28), ((0, 1), 30), ((1, 0), 31))
 TAPS_FROM = 28
 SMALL_AT = (36, 37, 39, 41)
-RED_AT = ((24, 26, 32, 35, 39), (31, 32, 37, 40, None))
+RED_AT = ((24, 26, 32, 35, 39), (31, 33, 38, 40, None))
 STEPS = 3 * HOPS + 2
 
 

time: 147 us -> 146 us (level)
  no operation moved by 1% of the time
where the time goes in v4:
time: 146 us; the launch traced here: 145 us
  Pallas kernels  145 us (99%)
    pallas_call x1, Pallas kernels, shards(): pl.pallas_call(body, out_shape=(jax.ShapeDtypeStruct((T + 2 * HALO, D), B...  140 us
    pallas_call x1, Pallas kernels, shards(): pl.pallas_call(finish, out_shape=(jax.ShapeDtypeStruct((1, T, D), BF16),...  4.88 us

profile of v4, /device:TPU:2, one launch (start us, length us, event | category | flops | bytes accessed | tf_op | source)
XLA Modules:
  0.0 145.2 jit_solution(17644774777043364983)
XLA Ops:
  0.6 139.7 %step.1 = (bf16[224,1280]{1,0:T(8,128)(2,1)}, bf16[320,1280]{1,0:T(8,128)(2,1)}, bf16[320,1280]{1,0:T(8,128)(2,1)}, f32[8,1280]{1,0:T(8,128)}) custom-call(bf16[1,192,1280]{2,1,0:T(8,128)(2,1)} %x_hbm.1, bf16[1,320,3072]{2,1,0:T(8,128)(2,1)} %bitcast.3, bf16[1,192,1280]{2,1,0:T(8,128)(2,1)} %u_hbm.1, bf16[320,1280]{1,0:T(8,128)(2,1)} %bitcast.4, ...), custom_call_target="tpu_custom_call" | custom-call | tf_op jit(solution)/shard_map/step/pallas_call | solution.py:704
  140.4 4.9 %finish.1 = (bf16[1,192,1280]{2,1,0:T(8,128)(2,1)}, f32[320,1280]{1,0:T(8,128)}, f32[320,1280]{1,0:T(8,128)}, f32[7,1280]{1,0:T(8,128)}, f32[320]{0:T(512)}) custom-call(bf16[224,1280]{1,0:T(8,128)(2,1)} %get-tuple-element.14.gm_hbm, bf16[320,1280]{1,0:T(8,128)(2,1)} %get-tuple-element.15.gwo_hbm, bf16[320,1280]{1,0:T(8,128)(2,1)} %get-tuple-element.16.gwi_hbm, ...), custom_call_target="tpu_custom_call" | custom-call | tf_op jit(solution)/shard_map/finish/pallas_call | solution.py:761
